TPU v7x, 32 devices: a whole 2x2x4 slice. The times are simulated.
32 devices in a mesh: tile: 8 (over y, x, core), pos: 4 (over z).
Axes of the slice: x: 2, y: 2, z: 4, core: 2. Of those that a mesh axis runs over, the one named last changes fastest.
Arguments:
- object_tiles: float32 [8, 2, 512, 512], P('tile'), may hold values from -5 to 5
- probe: float32 [2, 256, 256], replicated, may hold values from -6 to 6
- patterns: bfloat16 [256, 256, 256], P(('tile', 'pos')), may hold values from 0 to 4
- corners: int32 [256, 2], P(('tile', 'pos')), may hold values from 0 to 511, as said below
- counts: int32 [32], P(('tile', 'pos')), may hold values from 1 to 7, as said below
Outputs:
- refined: float32 [8, 2, 512, 512], P('tile')
Inputs may be any that keep to these rules, and one draw needn't show every extreme that they name: `corners`: tile t sits in grid cell (t + 8 + 8 // 2) mod 8 of a row-major grid of 8 tiles a row. A corner row is at most 256 for slots of tiles in the grid's last row, a corner column at most 256 for slots of tiles in the grid's last column, so every crop lies inside the object. The device at tile index t and the one at tile index t + 4 with the same pos index have counts that sum to exactly 8; some device has 7.
All inputs are finite; a program needn't handle non-finite values.
Results may differ from a plain program's by a relative error of at most 0.018.
Values may be sent and summed in bfloat16 or wider, within the bound.
No kernel may reach another device: no remote copies, remote signals or barrier semaphores. Data moves between devices by JAX's collectives and lax.ppermute only.
A program may use at most 64 MiB of HBM per device.

v0:
```python
import math

import jax
import jax.numpy as jnp
from jax import lax
from jax.sharding import PartitionSpec as P

TILE_COLS = 8
ITERS = 2


LEARNING_RATE = 0.03


def from_behind(value, axis, steps):
    count = lax.axis_size(axis)
    pairs = [(source, (source + steps) % count) for source in range(count)]
    return lax.ppermute(value, axis, pairs)


def tables(extent):
    counter = jnp.arange(extent, dtype=jnp.int32)
    phases = counter[:, None] * counter[None, :] % extent
    angles = phases.astype(jnp.float32) * (2.0 * math.pi / extent)
    factor = 1.0 / math.sqrt(extent)
    cosine = jnp.cos(angles) * factor
    sine_neg = -jnp.sin(angles) * factor
    forward_right = jnp.concatenate(
        [jnp.concatenate([cosine, sine_neg], 1), jnp.concatenate([-sine_neg, cosine], 1)], 0
    ).astype(jnp.bfloat16)
    forward_left = jnp.concatenate([cosine, sine_neg], 0).astype(jnp.bfloat16)
    backward_right = jnp.concatenate(
        [jnp.concatenate([cosine, -sine_neg], 1), jnp.concatenate([sine_neg, cosine], 1)], 0
    ).astype(jnp.bfloat16)
    backward_left = jnp.concatenate([cosine, -sine_neg], 0).astype(jnp.bfloat16)
    return (forward_right, forward_left, backward_right, backward_left)


def transform(waves, right_table, left_table):
    number, extent = (waves.shape[0], waves.shape[1])
    halfway = jnp.dot(
        waves.reshape(number * extent, 2 * extent), right_table, preferred_element_type=jnp.float32
    )
    halfway = halfway.reshape(number, extent, 2 * extent).astype(jnp.bfloat16)
    stacked = jnp.einsum("jk,skl->sjl", left_table, halfway, preferred_element_type=jnp.float32)
    upper = stacked[:, :extent]
    lower = stacked[:, extent:]
    real_part = upper[:, :, :extent] - lower[:, :, extent:]
    imag_part = upper[:, :, extent:] + lower[:, :, :extent]
    return jnp.concatenate([real_part, imag_part], 2)


def wave_gradient(waves, measured, table_set):
    extent = waves.shape[1]
    spectrum = transform(waves, table_set[0], table_set[1])
    power = spectrum[:, :, :extent] ** 2 + spectrum[:, :, extent:] ** 2
    misfit = power - measured.astype(jnp.float32)
    pushed = (spectrum * jnp.concatenate([misfit, misfit], 2)).astype(jnp.bfloat16)
    return transform(pushed, table_set[2], table_set[3]).astype(jnp.bfloat16)


def exit_waves(probe, crops):
    real_part = probe[0] * crops[:, 0] - probe[1] * crops[:, 1]
    imag_part = probe[0] * crops[:, 1] + probe[1] * crops[:, 0]
    return jnp.concatenate([real_part, imag_part], 2).astype(jnp.bfloat16)


def crop_gradients(probe, wave_grads, alive_mask):
    extent = probe.shape[1]
    real_in = wave_grads[:, :, :extent].astype(jnp.float32)
    imag_in = wave_grads[:, :, extent:].astype(jnp.float32)
    real_part = probe[0] * real_in + probe[1] * imag_in
    imag_part = probe[0] * imag_in - probe[1] * real_in
    return jnp.stack([real_part, imag_part], 1) * alive_mask[:, None, None, None]


def extend_tile(object_tile, keep_right, keep_down, extent):
    right_piece = from_behind(object_tile[:, :, :extent], "tile", -1) * keep_right
    lower_piece = (
        from_behind(object_tile[:, :extent, :].astype(jnp.bfloat16), "tile", -TILE_COLS).astype(
            jnp.float32
        )
        * keep_down
    )
    corner_piece = from_behind(
        object_tile[:, :extent, :extent].astype(jnp.bfloat16), "tile", -(TILE_COLS + 1)
    ).astype(jnp.float32) * (keep_right * keep_down)
    upper_band = jnp.concatenate([object_tile, right_piece], 2)
    lower_band = jnp.concatenate([lower_piece, corner_piece], 2)
    return jnp.concatenate([upper_band, lower_band], 1)


def fold_margins(extended_grad, keep_left, keep_up, extent, tile_edge):
    interior = extended_grad[:, :tile_edge, :tile_edge]
    right_in = (
        from_behind(
            extended_grad[:, :tile_edge, tile_edge:].astype(jnp.bfloat16), "tile", 1
        ).astype(jnp.float32)
        * keep_left
    )
    bottom_band = extended_grad[:, tile_edge:, :tile_edge]
    lower_in = (
        from_behind(bottom_band.astype(jnp.bfloat16), "tile", TILE_COLS).astype(bottom_band.dtype)
        * keep_up
    )
    interior = interior.at[:, :, :extent].add(right_in)
    interior = interior.at[:, :extent, :].add(lower_in)
    diagonal_in = from_behind(
        extended_grad[:, tile_edge:, tile_edge:].astype(jnp.bfloat16), "tile", TILE_COLS + 1
    ).astype(jnp.float32) * (keep_left * keep_up)
    interior = interior.at[:, :extent, :extent].add(diagonal_in)
    return interior


def shards(object_tiles, probe, patterns, corners, counts):
    object_tile = object_tiles[0]
    extent = probe.shape[1]
    tile_edge = object_tile.shape[1]
    slot_total = patterns.shape[0]
    table_set = tables(extent)
    tile_count = lax.axis_size("tile")
    grid_rows = tile_count // TILE_COLS
    cell_at = (lax.axis_index("tile") + TILE_COLS + TILE_COLS // 2) % tile_count
    column_at = cell_at % TILE_COLS
    row_at_grid = cell_at // TILE_COLS
    keep_right = (column_at != TILE_COLS - 1).astype(jnp.float32)
    keep_left = (column_at != 0).astype(jnp.float32)
    keep_down = (row_at_grid != grid_rows - 1).astype(jnp.float32)
    keep_up = (row_at_grid != 0).astype(jnp.float32)
    live_count = counts[0]
    slot_order = jnp.arange(slot_total, dtype=jnp.int32)
    alive_mask = (slot_order < live_count).astype(jnp.float32)
    corner_rows = corners[:, 0]
    corner_cols = corners[:, 1]
    zero_index = jnp.zeros((), jnp.int32)
    for repeat in range(ITERS):
        extended = extend_tile(object_tile, keep_right, keep_down, extent)

        def cut_window(row_at, col_at):
            return lax.dynamic_slice(extended, (zero_index, row_at, col_at), (2, extent, extent))

        crops = jax.vmap(cut_window)(corner_rows, corner_cols)
        waves = exit_waves(probe, crops)
        wave_grads = wave_gradient(waves, patterns, table_set)
        slot_grads = crop_gradients(probe, wave_grads, alive_mask)

        def add_slot(position, running):
            anchor = (zero_index, corner_rows[position], corner_cols[position])
            region = lax.dynamic_slice(running, anchor, (2, extent, extent))
            return lax.dynamic_update_slice(running, region + slot_grads[position], anchor)

        extended_grad = lax.fori_loop(
            0, slot_total, add_slot, jnp.zeros(extended.shape, jnp.float32)
        )
        tile_grad = fold_margins(extended_grad, keep_left, keep_up, extent, tile_edge)
        object_tile = object_tile - LEARNING_RATE * lax.psum(
            tile_grad.astype(jnp.bfloat16), "pos"
        ).astype(jnp.float32)
    return object_tile[None]


def solution(mesh):
    return jax.shard_map(
        shards,
        mesh=mesh,
        in_specs=(
            P("tile", None, None, None),
            P(),
            P(("tile", "pos"), None, None),
            P(("tile", "pos"), None),
            P(("tile", "pos")),
        ),
        out_specs=P("tile", None, None, None),
        check_vma=False,
    )
```

profile of v0, /device:TPU:0, one launch (start us, length us, event | category | flops | bytes accessed | tf_op | source)
XLA Modules:
  0.0 580.8 jit_solution(13232101011782488285)
XLA Ops:
  8.5 3.4 collective-permute-start.2
  14.5 4.7 collective-permute-start.1
  28.4 2.5 maximum_maximum_fusion
  30.9 2.5 broadcast.144.clone2
  33.4 34.4 %while.36 = (s32[]{:T(128)}, f32[2,768,768]{2,1,0:T(8,128)}, s32[8,3]{0,1:T(4,128)S(1)}, f32[8,2,256,256]{2,3,0,1:T(8,128)}, s32[]{:T(128)}) while((s32[]{:T(128)}, f32[2,768,768]{2,1,0:T(8,128)}, s32[8,3]{0,1:T(4,128)S(1)}, f32[8,2,256,256]{2,3,0,1:T(8,128)}, s32[]{:T(128)}) %tuple.123), condition=%wide.while_cond.6, body=%wide.while_body.6.sunk | while | flops 2 | bytes 3146353 | solution.py:140
  34.0 2.6 dynamic-slice_bitcast_fusion.4
  38.3 2.6 dynamic-slice_bitcast_fusion.4
  42.6 2.6 dynamic-slice_bitcast_fusion.4
  46.9 2.6 dynamic-slice_bitcast_fusion.4
  51.2 2.6 dynamic-slice_bitcast_fusion.4
  55.5 2.6 dynamic-slice_bitcast_fusion.4
  59.9 2.6 dynamic-slice_bitcast_fusion.4
  64.1 2.6 dynamic-slice_bitcast_fusion.4
  67.8 3.8 fusion.31
  71.6 7.0 %convolution_bitcast_fusion.3 = f32[8,512,512]{1,2,0:T(8,128)} fusion(bf16[8,256,256]{1,2,0:T(8,128)(2,1)} %get-tuple-element.354, bf16[8,256,256]{1,2,0:T(8,128)(2,1)S(1)} %get-tuple-element.353, bf16[256,256]{1,0:T(8,128)(2,1)S(1)} %get-tuple-element.362, bf16[256,256]{1,0:T(8,128)(2,1)S(1)} %get-tuple-element.361, bf16[256,256]{1,0:T(8,128)(2,1)S(1)} %fusion.80), kind=kOutput, calls=%fused_computation.21 | convolution fusion | flops 2155347968 | bytes 10878976 | tf_op jit(solution)/shard_map/jk,skl->sjl/dot_general | solution.py:45
  78.6 6.6 %convert_subtract_fusion.1 = (f32[8,256,256]{1,2,0:T(8,128)}, f32[8,256,256]{1,2,0:T(8,128)}, f32[8,256,256]{1,2,0:T(8,128)}) fusion(bf16[8,256,256]{1,2,0:T(8,128)(2,1)S(1)} %copy-done.3, f32[8,512,512]{1,2,0:T(8,128)} %convolution_bitcast_fusion.3), kind=kLoop, calls=%fused_computation.31 | loop fusion | flops 3670016 | bytes 15728640 | tf_op jit(solution)/shard_map/sub | solution.py:57
  85.2 9.2 %convolution_bitcast_fusion.2 = f32[8,512,512]{1,2,0:T(8,128)} fusion(f32[8,256,256]{1,2,0:T(8,128)} %get-tuple-element.346, f32[8,256,256]{1,2,0:T(8,128)} %get-tuple-element.345, f32[8,256,256]{1,2,0:T(8,128)} %get-tuple-element.344, bf16[256,256]{1,0:T(8,128)(2,1)S(1)} %get-tuple-element.362, bf16[256,256]{1,0:T(8,128)(2,1)S(1)} %fusion.80, ...), kind=kOutput, calls=%fused_computation.20 | convolution fusion | flops 2155347968 | bytes 15073280 | tf_op jit(solution)/shard_map/jk,skl->sjl/dot_general | solution.py:45
  94.4 4.4 fusion.3
  99.2 2.6 maximum_multiply_fusion.1
  101.8 2.4 broadcast.138.clone
  104.2 115.4 %while.34 = (s32[]{:T(128)}, f32[2,768,768]{2,1,0:T(8,128)}, s32[8]{0:T(128)S(1)}, s32[8]{0:T(128)S(1)}, f32[8,2,256,256]{2,3,0,1:T(8,128)}, /*index=5*/s32[]{:T(128)}, s32[]{:T(128)}, s32[]{:T(128)}) while((s32[]{:T(128)}, f32[2,768,768]{2,1,0:T(8,128)}, s32[8]{0:T(128)S(1)}, s32[8]{0:T(128)S(1)}, f32[8,2,256,256]{2,3,0,1:T(8,128)}, ...), condition=%wide.region_1.2_spmd, body=%wide.region_0.1_spmd.sunk | while | flops 131080 | bytes 4718785 | solution.py:152
  111.9 6.5 %dynamic_update_slice.16 = f32[2,768,768]{2,1,0:T(8,128)} dynamic-update-slice(f32[2,768,768]{2,1,0:T(8,128)} %get-tuple-element.507, f32[2,256,256]{2,1,0:T(8,128)S(1)} %bitcast_add_fusion.4, s32[]{:T(128)} %constant.250.clone.1..sunk, s32[]{:T(128)S(6)} %select_n.122, s32[]{:T(128)S(6)} %select_n.123) | dynamic-update-slice | bytes 1048580 | tf_op jit(solution)/shard_map/while/body/eval_jaxpr/dynamic_update_slice | solution.py:150
  126.2 6.5 %dynamic_update_slice.16 = f32[2,768,768]{2,1,0:T(8,128)} dynamic-update-slice(f32[2,768,768]{2,1,0:T(8,128)} %get-tuple-element.507, f32[2,256,256]{2,1,0:T(8,128)S(1)} %bitcast_add_fusion.4, s32[]{:T(128)} %constant.250.clone.1..sunk, s32[]{:T(128)S(6)} %select_n.122, s32[]{:T(128)S(6)} %select_n.123) | dynamic-update-slice | bytes 1048580 | tf_op jit(solution)/shard_map/while/body/eval_jaxpr/dynamic_update_slice | solution.py:150
  140.5 6.8 %dynamic_update_slice.16 = f32[2,768,768]{2,1,0:T(8,128)} dynamic-update-slice(f32[2,768,768]{2,1,0:T(8,128)} %get-tuple-element.507, f32[2,256,256]{2,1,0:T(8,128)S(1)} %bitcast_add_fusion.4, s32[]{:T(128)} %constant.250.clone.1..sunk, s32[]{:T(128)S(6)} %select_n.122, s32[]{:T(128)S(6)} %select_n.123) | dynamic-update-slice | bytes 1048580 | tf_op jit(solution)/shard_map/while/body/eval_jaxpr/dynamic_update_slice | solution.py:150
  155.0 6.5 %dynamic_update_slice.16 = f32[2,768,768]{2,1,0:T(8,128)} dynamic-update-slice(f32[2,768,768]{2,1,0:T(8,128)} %get-tuple-element.507, f32[2,256,256]{2,1,0:T(8,128)S(1)} %bitcast_add_fusion.4, s32[]{:T(128)} %constant.250.clone.1..sunk, s32[]{:T(128)S(6)} %select_n.122, s32[]{:T(128)S(6)} %select_n.123) | dynamic-update-slice | bytes 1048580 | tf_op jit(solution)/shard_map/while/body/eval_jaxpr/dynamic_update_slice | solution.py:150
  169.3 6.8 %dynamic_update_slice.16 = f32[2,768,768]{2,1,0:T(8,128)} dynamic-update-slice(f32[2,768,768]{2,1,0:T(8,128)} %get-tuple-element.507, f32[2,256,256]{2,1,0:T(8,128)S(1)} %bitcast_add_fusion.4, s32[]{:T(128)} %constant.250.clone.1..sunk, s32[]{:T(128)S(6)} %select_n.122, s32[]{:T(128)S(6)} %select_n.123) | dynamic-update-slice | bytes 1048580 | tf_op jit(solution)/shard_map/while/body/eval_jaxpr/dynamic_update_slice | solution.py:150
  183.8 6.8 %dynamic_update_slice.16 = f32[2,768,768]{2,1,0:T(8,128)} dynamic-update-slice(f32[2,768,768]{2,1,0:T(8,128)} %get-tuple-element.507, f32[2,256,256]{2,1,0:T(8,128)S(1)} %bitcast_add_fusion.4, s32[]{:T(128)} %constant.250.clone.1..sunk, s32[]{:T(128)S(6)} %select_n.122, s32[]{:T(128)S(6)} %select_n.123) | dynamic-update-slice | bytes 1048580 | tf_op jit(solution)/shard_map/while/body/eval_jaxpr/dynamic_update_slice | solution.py:150
  198.3 6.8 %dynamic_update_slice.16 = f32[2,768,768]{2,1,0:T(8,128)} dynamic-update-slice(f32[2,768,768]{2,1,0:T(8,128)} %get-tuple-element.507, f32[2,256,256]{2,1,0:T(8,128)S(1)} %bitcast_add_fusion.4, s32[]{:T(128)} %constant.250.clone.1..sunk, s32[]{:T(128)S(6)} %select_n.122, s32[]{:T(128)S(6)} %select_n.123) | dynamic-update-slice | bytes 1048580 | tf_op jit(solution)/shard_map/while/body/eval_jaxpr/dynamic_update_slice | solution.py:150
  212.8 6.7 %dynamic_update_slice.16 = f32[2,768,768]{2,1,0:T(8,128)} dynamic-update-slice(f32[2,768,768]{2,1,0:T(8,128)} %get-tuple-element.507, f32[2,256,256]{2,1,0:T(8,128)S(1)} %bitcast_add_fusion.4, s32[]{:T(128)} %constant.250.clone.1..sunk, s32[]{:T(128)S(6)} %select_n.122, s32[]{:T(128)S(6)} %select_n.123) | dynamic-update-slice | bytes 1048580 | tf_op jit(solution)/shard_map/while/body/eval_jaxpr/dynamic_update_slice | solution.py:150
  219.6 2.6 convert.80
  225.7 7.1 %collective-permute-done.3 = bf16[2,512,256]{2,1,0:T(8,128)(2,1)} collective-permute-done((bf16[2,512,256]{2,1,0:T(8,128)(2,1)}, bf16[2,512,256]{2,1,0:T(8,128)(2,1)}, u32[]{:S(2)}, u32[]{:S(2)}) %collective-permute-start.3) | collective-permute-done | bytes 524320 | tf_op jit(solution)/shard_map/ppermute | solution.py:18
  237.0 52.2 %all-reduce.3.cloned.1.call-done = bf16[2,512,512]{2,1,0:T(8,128)(2,1)} async-done(((bf16[2,512,512]{2,1,0:T(8,128)(2,1)}), bf16[2,512,512]{2,1,0:T(8,128)(2,1)}) %all-reduce.3.cloned.1.call-update) | async-done | bytes 1048592 | tf_op jit(solution)/shard_map/psum | solution.py:156
  295.5 4.7 collective-permute-start.7
  301.5 8.6 %collective-permute-done.8 = bf16[2,256,256]{2,1,0:T(8,128)(2,1)} collective-permute-done((bf16[2,256,256]{2,1,0:T(8,128)(2,1)}, bf16[2,256,256]{2,1,0:T(8,128)(2,1)}, u32[]{:S(2)}, u32[]{:S(2)}) %collective-permute-start.8) | collective-permute-done | bytes 262176 | tf_op jit(solution)/shard_map/ppermute | solution.py:18
  312.4 2.5 maximum_maximum_fusion.1
  314.9 2.5 broadcast.144.clone
  317.4 34.4 %while.37 = (s32[]{:T(128)}, f32[2,768,768]{2,1,0:T(8,128)}, s32[8,3]{0,1:T(4,128)S(1)}, f32[8,2,256,256]{2,3,0,1:T(8,128)}, s32[]{:T(128)}) while((s32[]{:T(128)}, f32[2,768,768]{2,1,0:T(8,128)}, s32[8,3]{0,1:T(4,128)S(1)}, f32[8,2,256,256]{2,3,0,1:T(8,128)}, s32[]{:T(128)}) %tuple.139), condition=%wide.while_cond.7, body=%wide.while_body.7.sunk | while | flops 2 | bytes 3146353 | solution.py:140
  318.0 2.6 dynamic-slice_bitcast_fusion.5
  322.2 2.6 dynamic-slice_bitcast_fusion.5
  326.5 2.6 dynamic-slice_bitcast_fusion.5
  330.8 2.6 dynamic-slice_bitcast_fusion.5
  335.1 2.6 dynamic-slice_bitcast_fusion.5
  339.5 2.6 dynamic-slice_bitcast_fusion.5
  343.8 2.6 dynamic-slice_bitcast_fusion.5
  348.1 2.6 dynamic-slice_bitcast_fusion.5
  351.8 4.1 fusion.27
  355.9 7.4 %convolution_bitcast_fusion.1 = f32[8,512,512]{1,2,0:T(8,128)} fusion(bf16[8,256,256]{1,2,0:T(8,128)(2,1)} %get-tuple-element.352, bf16[8,256,256]{1,2,0:T(8,128)(2,1)} %get-tuple-element.351, bf16[256,256]{1,0:T(8,128)(2,1)S(1)} %get-tuple-element.362, bf16[256,256]{1,0:T(8,128)(2,1)} %copy-done.6, bf16[256,256]{1,0:T(8,128)(2,1)} %copy-done.5), kind=kOutput, calls=%fused_computation.19 | convolution fusion | flops 2155347968 | bytes 10878976 | tf_op jit(solution)/shard_map/jk,skl->sjl/dot_general | solution.py:45
  363.3 6.6 %convert_subtract_fusion = (f32[8,256,256]{1,2,0:T(8,128)}, f32[8,256,256]{1,2,0:T(8,128)}, f32[8,256,256]{1,2,0:T(8,128)}) fusion(bf16[8,256,256]{1,2,0:T(8,128)(2,1)S(1)} %copy-done.4, f32[8,512,512]{1,2,0:T(8,128)} %convolution_bitcast_fusion.1), kind=kLoop, calls=%fused_computation.30 | loop fusion | flops 3670016 | bytes 15728640 | tf_op jit(solution)/shard_map/sub | solution.py:57
  369.9 9.3 %convolution_bitcast_fusion = f32[8,512,512]{1,2,0:T(8,128)} fusion(f32[8,256,256]{1,2,0:T(8,128)} %get-tuple-element.336, f32[8,256,256]{1,2,0:T(8,128)} %get-tuple-element.335, f32[8,256,256]{1,2,0:T(8,128)} %get-tuple-element.334, bf16[256,256]{1,0:T(8,128)(2,1)S(1)} %get-tuple-element.362, bf16[256,256]{1,0:T(8,128)(2,1)} %copy-done.5, ...), kind=kOutput, calls=%fused_computation.18 | convolution fusion | flops 2155347968 | bytes 15073280 | tf_op jit(solution)/shard_map/jk,skl->sjl/dot_general | solution.py:45
  379.1 4.4 fusion.7
  383.9 2.6 maximum_multiply_fusion.3
  388.9 115.4 %while.35 = (s32[]{:T(128)}, f32[2,768,768]{2,1,0:T(8,128)}, s32[8]{0:T(128)S(1)}, s32[8]{0:T(128)S(1)}, f32[8,2,256,256]{2,3,0,1:T(8,128)}, /*index=5*/s32[]{:T(128)}, s32[]{:T(128)}, s32[]{:T(128)}) while((s32[]{:T(128)}, f32[2,768,768]{2,1,0:T(8,128)}, s32[8]{0:T(128)S(1)}, s32[8]{0:T(128)S(1)}, f32[8,2,256,256]{2,3,0,1:T(8,128)}, ...), condition=%wide.region_4.5_spmd, body=%wide.region_3.4_spmd.sunk | while | flops 131080 | bytes 4718785 | solution.py:152
  396.6 6.5 %dynamic_update_slice.17 = f32[2,768,768]{2,1,0:T(8,128)} dynamic-update-slice(f32[2,768,768]{2,1,0:T(8,128)} %get-tuple-element.546, f32[2,256,256]{2,1,0:T(8,128)S(1)} %bitcast_add_fusion.5, s32[]{:T(128)} %constant.250.clone.1..sunk.1, s32[]{:T(128)S(6)} %select_n.124, s32[]{:T(128)S(6)} %select_n.125) | dynamic-update-slice | bytes 1048580 | tf_op jit(solution)/shard_map/while/body/eval_jaxpr/dynamic_update_slice | solution.py:150
  410.9 6.5 %dynamic_update_slice.17 = f32[2,768,768]{2,1,0:T(8,128)} dynamic-update-slice(f32[2,768,768]{2,1,0:T(8,128)} %get-tuple-element.546, f32[2,256,256]{2,1,0:T(8,128)S(1)} %bitcast_add_fusion.5, s32[]{:T(128)} %constant.250.clone.1..sunk.1, s32[]{:T(128)S(6)} %select_n.124, s32[]{:T(128)S(6)} %select_n.125) | dynamic-update-slice | bytes 1048580 | tf_op jit(solution)/shard_map/while/body/eval_jaxpr/dynamic_update_slice | solution.py:150
  425.2 6.8 %dynamic_update_slice.17 = f32[2,768,768]{2,1,0:T(8,128)} dynamic-update-slice(f32[2,768,768]{2,1,0:T(8,128)} %get-tuple-element.546, f32[2,256,256]{2,1,0:T(8,128)S(1)} %bitcast_add_fusion.5, s32[]{:T(128)} %constant.250.clone.1..sunk.1, s32[]{:T(128)S(6)} %select_n.124, s32[]{:T(128)S(6)} %select_n.125) | dynamic-update-slice | bytes 1048580 | tf_op jit(solution)/shard_map/while/body/eval_jaxpr/dynamic_update_slice | solution.py:150
  439.7 6.5 %dynamic_update_slice.17 = f32[2,768,768]{2,1,0:T(8,128)} dynamic-update-slice(f32[2,768,768]{2,1,0:T(8,128)} %get-tuple-element.546, f32[2,256,256]{2,1,0:T(8,128)S(1)} %bitcast_add_fusion.5, s32[]{:T(128)} %constant.250.clone.1..sunk.1, s32[]{:T(128)S(6)} %select_n.124, s32[]{:T(128)S(6)} %select_n.125) | dynamic-update-slice | bytes 1048580 | tf_op jit(solution)/shard_map/while/body/eval_jaxpr/dynamic_update_slice | solution.py:150
  454.0 6.8 %dynamic_update_slice.17 = f32[2,768,768]{2,1,0:T(8,128)} dynamic-update-slice(f32[2,768,768]{2,1,0:T(8,128)} %get-tuple-element.546, f32[2,256,256]{2,1,0:T(8,128)S(1)} %bitcast_add_fusion.5, s32[]{:T(128)} %constant.250.clone.1..sunk.1, s32[]{:T(128)S(6)} %select_n.124, s32[]{:T(128)S(6)} %select_n.125) | dynamic-update-slice | bytes 1048580 | tf_op jit(solution)/shard_map/while/body/eval_jaxpr/dynamic_update_slice | solution.py:150
  468.5 6.8 %dynamic_update_slice.17 = f32[2,768,768]{2,1,0:T(8,128)} dynamic-update-slice(f32[2,768,768]{2,1,0:T(8,128)} %get-tuple-element.546, f32[2,256,256]{2,1,0:T(8,128)S(1)} %bitcast_add_fusion.5, s32[]{:T(128)} %constant.250.clone.1..sunk.1, s32[]{:T(128)S(6)} %select_n.124, s32[]{:T(128)S(6)} %select_n.125) | dynamic-update-slice | bytes 1048580 | tf_op jit(solution)/shard_map/while/body/eval_jaxpr/dynamic_update_slice | solution.py:150
  483.0 6.8 %dynamic_update_slice.17 = f32[2,768,768]{2,1,0:T(8,128)} dynamic-update-slice(f32[2,768,768]{2,1,0:T(8,128)} %get-tuple-element.546, f32[2,256,256]{2,1,0:T(8,128)S(1)} %bitcast_add_fusion.5, s32[]{:T(128)} %constant.250.clone.1..sunk.1, s32[]{:T(128)S(6)} %select_n.124, s32[]{:T(128)S(6)} %select_n.125) | dynamic-update-slice | bytes 1048580 | tf_op jit(solution)/shard_map/while/body/eval_jaxpr/dynamic_update_slice | solution.py:150
  497.5 6.7 %dynamic_update_slice.17 = f32[2,768,768]{2,1,0:T(8,128)} dynamic-update-slice(f32[2,768,768]{2,1,0:T(8,128)} %get-tuple-element.546, f32[2,256,256]{2,1,0:T(8,128)S(1)} %bitcast_add_fusion.5, s32[]{:T(128)} %constant.250.clone.1..sunk.1, s32[]{:T(128)S(6)} %select_n.124, s32[]{:T(128)S(6)} %select_n.125) | dynamic-update-slice | bytes 1048580 | tf_op jit(solution)/shard_map/while/body/eval_jaxpr/dynamic_update_slice | solution.py:150
  504.3 2.7 convert.84
  508.3 8.2 %collective-permute-done.9 = bf16[2,512,256]{2,1,0:T(8,128)(2,1)S(1)} collective-permute-done((bf16[2,512,256]{2,1,0:T(8,128)(2,1)S(1)}, bf16[2,512,256]{2,1,0:T(8,128)(2,1)S(1)}, u32[]{:S(2)}, u32[]{:S(2)}) %collective-permute-start.9) | collective-permute-done | bytes 524320 | tf_op jit(solution)/shard_map/ppermute | solution.py:18
  520.6 50.4 %all-reduce.5.cloned.1.call-done = bf16[2,512,512]{2,1,0:T(8,128)(2,1)} async-done(((bf16[2,512,512]{2,1,0:T(8,128)(2,1)}), bf16[2,512,512]{2,1,0:T(8,128)(2,1)}) %all-reduce.5.cloned.1.call-update) | async-done | bytes 1048592 | tf_op jit(solution)/shard_map/psum | solution.py:156
  571.1 2.9 subtract_bitcast_fusion
  (232 shorter events, 126.6 us)
Async XLA Ops:
  6.5 5.3 copy-start
  6.5 282.8 %all-reduce.3.cloned.1.call-start = ((), (), s32[]{:S(2)}) async-start(), calls=%async_computation | async-start | bytes 2097152 | tf_op jit(solution)/shard_map/psum | solution.py:156
  8.4 10.8 %copy-start.8 = (s32[8,2]{0,1:T(2,128)S(1)}, s32[8,2]{0,1:T(2,128)}, u32[]{:S(2)}) copy-start(s32[8,2]{0,1:T(2,128)} %param.24) | copy-start | bytes 196
  8.4 11.4 %copy-start.7 = (f32[2,256,256]{2,1,0:T(8,128)S(1)}, f32[2,256,256]{2,1,0:T(8,128)}, u32[]{:S(2)}) copy-start(f32[2,256,256]{2,1,0:T(8,128)} %param.22) | copy-start | bytes 1572868
  8.5 16.3 %collective-permute-start.2 = (bf16[2,256,256]{2,1,0:T(8,128)(2,1)S(1)}, bf16[2,256,256]{2,1,0:T(8,128)(2,1)}, u32[]{:S(2)}, u32[]{:S(2)}) collective-permute-start(bf16[2,256,256]{2,1,0:T(8,128)(2,1)S(1)} %slice.414), channel_id=1, source_target_pairs={{0,28},{4,0},{8,4},{12,8},{16,12},{20,16},{24,20},{28,24},{1,29},{... | collective-permute-start | bytes 786440 | tf_op jit(solution)/shard_map/ppermute | solution.py:18
  13.0 14.2 %collective-permute-start = (f32[2,512,256]{2,1,0:T(8,128)}, f32[2,512,256]{2,1,0:T(8,128)}, u32[]{:S(2)}, u32[]{:S(2)}) collective-permute-start(f32[2,512,256]{2,1,0:T(8,128)} %slice.412), channel_id=1, source_target_pairs={{0,28},{4,0},{8,4},{12,8},{16,12},{20,16},{24,20},{28,24},{1,29},{... | collective-permute-start | bytes 3145736 | tf_op jit(solution)/shard_map/ppermute | solution.py:18
  14.5 11.4 %collective-permute-start.1 = (bf16[2,256,512]{2,1,0:T(8,128)(2,1)}, bf16[2,256,512]{2,1,0:T(8,128)(2,1)}, u32[]{:S(2)}, u32[]{:S(2)}) collective-permute-start(bf16[2,256,512]{2,1,0:T(8,128)(2,1)} %slice.413), channel_id=1, source_target_pairs={{0,0},{4,4},{8,8},{12,12},{16,16},{20,20},{24,24},{28,28},{1,1},{5... | collective-permute-start | bytes 1572872 | tf_op jit(solution)/shard_map/ppermute | solution.py:18
  20.2 78.6 %copy-start.1 = (f32[256,256]{0,1:T(8,128)}, f32[256,256]{0,1:T(8,128)S(1)}, u32[]{:S(2)}) copy-start(f32[256,256]{0,1:T(8,128)S(1)} %copy.8) | copy-start | bytes 786436
  23.6 61.6 %copy-start.5 = (bf16[256,256]{1,0:T(8,128)(2,1)}, bf16[256,256]{1,0:T(8,128)(2,1)S(1)}, u32[]{:S(2)}) copy-start(bf16[256,256]{1,0:T(8,128)(2,1)S(1)} %fusion.80) | copy-start | bytes 393220
  24.8 60.5 %copy-start.6 = (bf16[256,256]{1,0:T(8,128)(2,1)}, bf16[256,256]{1,0:T(8,128)(2,1)S(1)}, u32[]{:S(2)}) copy-start(bf16[256,256]{1,0:T(8,128)(2,1)S(1)} %get-tuple-element.361) | copy-start | bytes 393220
  71.6 7.0 %copy-start.3 = (bf16[8,256,256]{1,2,0:T(8,128)(2,1)S(1)}, bf16[8,256,256]{1,2,0:T(8,128)(2,1)}, u32[]{:S(2)}) copy-start(bf16[8,256,256]{1,2,0:T(8,128)(2,1)} %copy.10) | copy-start | bytes 3145732
  223.0 9.8 %collective-permute-start.3 = (bf16[2,512,256]{2,1,0:T(8,128)(2,1)}, bf16[2,512,256]{2,1,0:T(8,128)(2,1)}, u32[]{:S(2)}, u32[]{:S(2)}) collective-permute-start(bf16[2,512,256]{2,1,0:T(8,128)(2,1)} %slice.423), channel_id=1, source_target_pairs={{0,4},{4,8},{8,12},{12,16},{16,20},{20,24},{24,28},{28,0},{1,5},{5... | collective-permute-start | bytes 1572872 | tf_op jit(solution)/shard_map/ppermute | solution.py:18
  223.0 11.3 %collective-permute-start.4 = (bf16[2,256,512]{2,1,0:T(8,128)(2,1)S(1)}, bf16[2,256,512]{2,1,0:T(8,128)(2,1)}, u32[]{:S(2)}, u32[]{:S(2)}) collective-permute-start(bf16[2,256,512]{2,1,0:T(8,128)(2,1)S(1)} %slice.425), channel_id=1, source_target_pairs={{0,0},{4,4},{8,8},{12,12},{16,16},{20,20},{24,24},{28,28},{1,1},{5... | collective-permute-start | bytes 1572872 | tf_op jit(solution)/shard_map/ppermute | solution.py:18
  225.6 10.2 %collective-permute-start.5 = (bf16[2,256,256]{2,1,0:T(8,128)(2,1)S(1)}, bf16[2,256,256]{2,1,0:T(8,128)(2,1)S(1)}, u32[]{:S(2)}, u32[]{:S(2)}) collective-permute-start(bf16[2,256,256]{2,1,0:T(8,128)(2,1)S(1)} %slice.427), channel_id=1, source_target_pairs={{0,4},{4,8},{8,12},{12,16},{16,20},{20,24},{24,28},{28,0},{1,5},{5... | collective-permute-start | bytes 786440 | tf_op jit(solution)/shard_map/ppermute | solution.py:18
  237.0 334.1 %all-reduce.5.cloned.1.call-start = ((), (), s32[]{:S(2)}) async-start(), calls=%async_computation.1 | async-start | bytes 2097152 | tf_op jit(solution)/shard_map/psum | solution.py:156
  292.7 19.6 %collective-permute-start.6 = (f32[2,512,256]{2,1,0:T(8,128)}, f32[2,512,256]{2,1,0:T(8,128)S(1)}, u32[]{:S(2)}, u32[]{:S(2)}) collective-permute-start(f32[2,512,256]{2,1,0:T(8,128)} %slice.428), channel_id=1, source_target_pairs={{0,28},{4,0},{8,4},{12,8},{16,12},{20,16},{24,20},{28,24},{1,29},{... | collective-permute-start | bytes 3145736 | tf_op jit(solution)/shard_map/ppermute | solution.py:18
  295.5 15.6 %collective-permute-start.7 = (bf16[2,256,512]{2,1,0:T(8,128)(2,1)}, bf16[2,256,512]{2,1,0:T(8,128)(2,1)}, u32[]{:S(2)}, u32[]{:S(2)}) collective-permute-start(bf16[2,256,512]{2,1,0:T(8,128)(2,1)} %slice.429), channel_id=1, source_target_pairs={{0,0},{4,4},{8,8},{12,12},{16,16},{20,20},{24,24},{28,28},{1,1},{5... | collective-permute-start | bytes 1572872 | tf_op jit(solution)/shard_map/ppermute | solution.py:18
  300.9 9.2 %collective-permute-start.8 = (bf16[2,256,256]{2,1,0:T(8,128)(2,1)}, bf16[2,256,256]{2,1,0:T(8,128)(2,1)}, u32[]{:S(2)}, u32[]{:S(2)}) collective-permute-start(bf16[2,256,256]{2,1,0:T(8,128)(2,1)} %slice.430), channel_id=1, source_target_pairs={{0,28},{4,0},{8,4},{12,8},{16,12},{20,16},{24,20},{28,24},{1,29},{... | collective-permute-start | bytes 786440 | tf_op jit(solution)/shard_map/ppermute | solution.py:18
  355.9 7.4 %copy-start.4 = (bf16[8,256,256]{1,2,0:T(8,128)(2,1)S(1)}, bf16[8,256,256]{1,2,0:T(8,128)(2,1)}, u32[]{:S(2)}) copy-start(bf16[8,256,256]{1,2,0:T(8,128)(2,1)} %copy.10) | copy-start | bytes 3145732
  369.9 9.3 %copy-start.2 = (f32[256,256]{0,1:T(8,128)S(1)}, f32[256,256]{0,1:T(8,128)}, u32[]{:S(2)}) copy-start(f32[256,256]{0,1:T(8,128)} %copy-done.1) | copy-start | bytes 786436
  504.3 3.6 slice-start
  504.3 3.7 slice-start.1
  507.0 9.6 %collective-permute-start.9 = (bf16[2,512,256]{2,1,0:T(8,128)(2,1)S(1)}, bf16[2,512,256]{2,1,0:T(8,128)(2,1)S(1)}, u32[]{:S(2)}, u32[]{:S(2)}) collective-permute-start(bf16[2,512,256]{2,1,0:T(8,128)(2,1)S(1)} %slice.439), channel_id=1, source_target_pairs={{0,4},{4,8},{8,12},{12,16},{16,20},{20,24},{24,28},{28,0},{1,5},{5... | collective-permute-start | bytes 1572872 | tf_op jit(solution)/shard_map/ppermute | solution.py:18
  507.1 9.6 %collective-permute-start.10 = (bf16[2,256,512]{2,1,0:T(8,128)(2,1)S(1)}, bf16[2,256,512]{2,1,0:T(8,128)(2,1)S(1)}, u32[]{:S(2)}, u32[]{:S(2)}) collective-permute-start(bf16[2,256,512]{2,1,0:T(8,128)(2,1)S(1)} %slice.441), channel_id=1, source_target_pairs={{0,0},{4,4},{8,8},{12,12},{16,16},{20,20},{24,24},{28,28},{1,1},{5... | collective-permute-start | bytes 1572872 | tf_op jit(solution)/shard_map/ppermute | solution.py:18
  508.3 11.1 %collective-permute-start.11 = (bf16[2,256,256]{2,1,0:T(8,128)(2,1)S(1)}, bf16[2,256,256]{2,1,0:T(8,128)(2,1)S(1)}, u32[]{:S(2)}, u32[]{:S(2)}) collective-permute-start(bf16[2,256,256]{2,1,0:T(8,128)(2,1)S(1)} %slice.443), channel_id=1, source_target_pairs={{0,4},{4,8},{8,12},{12,16},{16,20},{20,24},{24,28},{28,0},{1,5},{5... | collective-permute-start | bytes 786440 | tf_op jit(solution)/shard_map/ppermute | solution.py:18
Sparse Core Ops, SparseCore 0:
  237.1 52.1 all-reduce.2
  520.7 50.2 all-reduce.4
where the time goes:
time: 587 us; the launch traced here: 581 us
  local copies, waits for them, and re-layouts  236 us (40%)
  waiting for transfers between devices  129 us (22%)
  other arithmetic  88.9 us (15%)
  loops' own time  62.6 us (11%)
  matrix products  32.8 us (6%)
  starting transfers between devices  17 us (3%)
  between operations  14.5 us (2%)
    dynamic_update_slice x16, local copies, waits for them, and re-layouts, add_slot(): lax.dynamic_update_slice(running, region + slot_grads[position], anchor)  107 us
    psum x2, waiting for transfers between devices, shards(): lax.psum(tile_grad.astype(jnp.bfloat16), 'pos').astype(jnp.float32)  103 us
    gather x80, local copies, waits for them, and re-layouts  68.7 us
    another operation x2, loops' own time, shards(): lax.fori_loop(0, slot_total, add_slot, jnp.zeros(extended.shape, jnp.floa...  62.5 us
    dot_general x4, matrix products, transform(): jnp.einsum('jk,skl->sjl', left_table, halfway, preferred_element_type=jnp...  32.8 us
    ppermute x12, waiting for transfers between devices, from_behind(): return lax.ppermute(value, axis, pairs)  26.4 us
    add x16, other arithmetic, add_slot(): region + slot_grads[position]  21.9 us
    dynamic_slice x32, local copies, waits for them, and re-layouts, add_slot(): slot_grads[position]  20.5 us
  transfers between devices with their start and end apart: 14, of which 7 were waited for; matrix products, arithmetic and copies ran while one was open for 3% of the time, Pallas kernels for 0%

commit v1 on v0

v1 whole, which is shorter than its diff:
```python
import functools
import math

import jax
import jax.numpy as jnp
import numpy as np
from jax import lax
from jax.experimental import pallas as pl
from jax.experimental.pallas import tpu as pltpu
from jax.sharding import PartitionSpec as P

TILE_COLS = 8
ITERS = 2
LEARNING_RATE = 0.03
LANES = 128
SUBLANES = 8
VMEM = pltpu.VMEM
SMEM = pltpu.SMEM


def tables(extent):
    counter = np.arange(extent)
    angles = (counter[:, None] * counter[None, :] % extent) * (2.0 * math.pi / extent)
    cosine = np.cos(angles) / math.sqrt(extent)
    sine_neg = -np.sin(angles) / math.sqrt(extent)
    cosine, sine_neg = (jnp.asarray(v, jnp.float32).astype(jnp.bfloat16) for v in (cosine, sine_neg))
    first = jnp.concatenate(
        [jnp.concatenate([cosine, sine_neg], 1), jnp.concatenate([-sine_neg, cosine], 1)], 0
    )
    second = jnp.concatenate(
        [jnp.concatenate([cosine, -sine_neg], 1), jnp.concatenate([sine_neg, cosine], 1)], 0
    )
    return first, second


def transform(side_by_side, right_table, left_table):
    extent = side_by_side.shape[0]
    halfway = jnp.dot(side_by_side, right_table, preferred_element_type=jnp.float32).astype(
        jnp.bfloat16
    )
    stacked = jnp.concatenate([halfway[:, :extent], halfway[:, extent:]], 0)
    return jnp.dot(left_table, stacked, preferred_element_type=jnp.float32)


def visit_slots(corners, counts, probe, patterns, first, second, extended, grad):
    extent = patterns.shape[1]
    rows_iota = lax.broadcasted_iota(jnp.int32, (SUBLANES, LANES), 0)
    lane_iota = lax.broadcasted_iota(jnp.int32, (extent, LANES), 1)

    def visit(slot, carry):
        row_at = corners[slot, 0]
        col_at = corners[slot, 1]
        row_base = pl.multiple_of(row_at // SUBLANES * SUBLANES, SUBLANES)
        col_base = pl.multiple_of(col_at // LANES * LANES, LANES)
        row_turn = row_at - row_base
        col_turn = col_at - col_base
        col_next = pl.multiple_of(col_base + LANES, LANES)
        col_wrap = pl.multiple_of(col_base + extent, LANES)
        row_wrap = pl.multiple_of(row_base + extent, SUBLANES)
        wrapped_lane = lane_iota < col_turn
        wrapped_row = rows_iota < row_turn

        def column(plane, col):
            body = extended[plane, pl.ds(row_base, extent), pl.ds(col, LANES)]
            tail = extended[plane, pl.ds(row_wrap, SUBLANES), pl.ds(col, LANES)]
            top = jnp.where(wrapped_row, tail, body[:SUBLANES])
            return jnp.concatenate([top, body[SUBLANES:]], 0)

        def window(plane):
            left = jnp.where(wrapped_lane, column(plane, col_wrap), column(plane, col_base))
            return jnp.concatenate([left, column(plane, col_next)], 1)

        def turned(plane):
            return pltpu.roll(pltpu.roll(probe[plane], row_turn, 0), col_turn, 1)

        probe_re = turned(0)
        probe_im = turned(1)
        crop_re = window(0)
        crop_im = window(1)
        wave = jnp.concatenate(
            [
                (probe_re * crop_re - probe_im * crop_im).astype(jnp.bfloat16),
                (probe_re * crop_im + probe_im * crop_re).astype(jnp.bfloat16),
            ],
            1,
        )
        spectrum = transform(wave, first[...], second[...])
        real = spectrum[:extent]
        imag = spectrum[extent:]
        misfit = real * real + imag * imag - patterns[slot].astype(jnp.float32)
        pushed = jnp.concatenate(
            [(misfit * real).astype(jnp.bfloat16), (misfit * imag).astype(jnp.bfloat16)], 1
        )
        wave_grad = transform(pushed, second[...], first[...]).astype(jnp.bfloat16)
        grad_re = wave_grad[:extent].astype(jnp.float32)
        grad_im = wave_grad[extent:].astype(jnp.float32)

        def add_column(plane, col, value):
            body = pl.ds(pl.multiple_of(row_base + SUBLANES, SUBLANES), extent - SUBLANES)
            grad[plane, body, pl.ds(col, LANES)] += value[SUBLANES:]
            top = value[:SUBLANES]
            grad[plane, pl.ds(row_base, SUBLANES), pl.ds(col, LANES)] += jnp.where(
                wrapped_row, 0.0, top
            )
            grad[plane, pl.ds(row_wrap, SUBLANES), pl.ds(col, LANES)] += jnp.where(
                wrapped_row, top, 0.0
            )

        def add_window(plane, value):
            left = value[:, :LANES]
            add_column(plane, col_base, jnp.where(wrapped_lane, 0.0, left))
            add_column(plane, col_next, value[:, LANES:])
            add_column(plane, col_wrap, jnp.where(wrapped_lane, left, 0.0))

        add_window(0, probe_re * grad_re + probe_im * grad_im)
        add_window(1, probe_re * grad_im - probe_im * grad_re)
        return carry

    lax.fori_loop(0, counts[0], visit, 0)


def row_kernel(
    with_update,
    corners,
    counts,
    plane_index,
    tile,
    margin,
    probe,
    patterns,
    first,
    second,
    *rest,
):
    if with_update:
        left_own, left_other, right_own, right_other, margin_own, margin_other, *rest = rest
    (
        left_send,
        left_keep,
        margin_send,
        margin_cross,
        right_send,
        right_keep,
        *rest,
    ) = rest
    if with_update:
        tile_out, *rest = rest
    extended, grad = rest
    extent = probe.shape[1]
    edge = tile.shape[1]
    own = plane_index[0]
    other = 1 - own
    if with_update:
        for plane, pieces in (
            (own, (left_own, right_own, margin_own)),
            (other, (left_other, right_other, margin_other)),
        ):
            for block, piece in enumerate(pieces):
                step = LEARNING_RATE * piece[...].astype(jnp.float32)
                cols = slice(block * extent, (block + 1) * extent)
                if block * extent < edge:
                    value = tile[plane, :, cols] - step
                    tile_out[plane, :, cols] = value
                else:
                    value = margin[plane].astype(jnp.float32) - step
                extended[plane, :edge, cols] = value
    else:
        for plane in (0, 1):
            extended[plane, :edge, :edge] = tile[plane]
            extended[plane, :edge, edge:] = margin[plane].astype(jnp.float32)
    grad[...] = jnp.zeros_like(grad)
    visit_slots(corners, counts, probe, patterns, first, second, extended, grad)
    left = slice(0, extent)
    right = slice(extent, edge)
    beyond = slice(edge, edge + extent)
    left_send[...] = grad[other, :edge, left].astype(jnp.bfloat16)
    left_keep[...] = grad[own, :edge, left]
    margin_send[...] = grad[own, :edge, beyond].astype(jnp.bfloat16)
    margin_cross[...] = grad[other, :edge, beyond].astype(jnp.bfloat16)
    right_send[...] = grad[other, :edge, right].astype(jnp.bfloat16)
    right_keep[...] = grad[own, :edge, right]


def row_step(corners, counts, plane_index, tile, margin, probe, patterns, table_set, pieces):
    extent = probe.shape[1]
    edge = tile.shape[1]
    slots = patterns.shape[0]
    half = jax.ShapeDtypeStruct((edge, extent), jnp.bfloat16)
    wide = jax.ShapeDtypeStruct((edge, extent), jnp.float32)
    outs = [half, wide, half, half, half, wide]
    if pieces:
        outs.append(jax.ShapeDtypeStruct(tile.shape, jnp.float32))
    whole = pl.BlockSpec(memory_space=VMEM)
    scalar = pl.BlockSpec(memory_space=SMEM)
    return pl.pallas_call(
        functools.partial(row_kernel, bool(pieces)),
        out_shape=outs,
        in_specs=[scalar] * 3 + [whole] * (6 + len(pieces)),
        out_specs=[whole] * len(outs),
        scratch_shapes=[
            pltpu.VMEM((2, edge + SUBLANES, edge + extent), jnp.float32),
            pltpu.VMEM((2, edge + SUBLANES, edge + extent), jnp.float32),
        ],
        cost_estimate=pl.CostEstimate(
            flops=slots * 32 * extent**3, bytes_accessed=8 * edge * edge, transcendentals=0
        ),
        compiler_params=pltpu.CompilerParams(vmem_limit_bytes=40 << 20),
    )(corners, counts, plane_index, tile, margin, probe, patterns, *table_set, *pieces)


def finish_kernel(plane_index, tile, left_own, left_other, right_own, right_other, out):
    own = plane_index[0]
    extent = left_own.shape[1]
    for plane, pieces in ((own, (left_own, right_own)), (1 - own, (left_other, right_other))):
        for block, piece in enumerate(pieces):
            cols = slice(block * extent, (block + 1) * extent)
            step = LEARNING_RATE * piece[...].astype(jnp.float32)
            out[plane, :, cols] = tile[plane, :, cols] - step


def finish(plane_index, tile, pieces):
    whole = pl.BlockSpec(memory_space=VMEM)
    return pl.pallas_call(
        finish_kernel,
        out_shape=jax.ShapeDtypeStruct(tile.shape, jnp.float32),
        in_specs=[pl.BlockSpec(memory_space=SMEM)] + [whole] * 5,
        out_specs=whole,
    )(plane_index, tile, *pieces)


def tile_pairs(count, row_shift, col_shift, grid_rows):
    turn = TILE_COLS + TILE_COLS // 2
    pairs = []
    for source in range(count):
        cell = (source + turn) % count
        row = cell // TILE_COLS + row_shift
        col = cell % TILE_COLS + col_shift
        if 0 <= row < grid_rows and 0 <= col < TILE_COLS:
            pairs.append((source, (row * TILE_COLS + col - turn) % count))
    return pairs


def move(value, pairs, sharers, mask):
    both = [
        (source * sharers + pos, target * sharers + (pos ^ mask))
        for source, target in pairs
        for pos in range(sharers)
    ]
    return lax.ppermute(value, ("tile", "pos"), both)


def row_shards(object_tile, probe, patterns, corners, counts, table_set):
    tile_count = lax.axis_size("tile")
    sharers = lax.axis_size("pos")
    extent = probe.shape[1]
    here = [(tile, tile) for tile in range(tile_count)]
    onward = tile_pairs(tile_count, 0, 1, 1)
    back = tile_pairs(tile_count, 0, -1, 1)
    plane_index = (lax.axis_index("pos") % 2).reshape(1).astype(jnp.int32)
    margin = move(object_tile[:, :, :extent].astype(jnp.bfloat16), back, sharers, 0)
    total = lambda *values: sum(value.astype(jnp.float32) for value in values).astype(jnp.bfloat16)
    pieces = ()
    for repeat in range(ITERS):
        left_send, left_keep, margin_send, margin_cross, right_send, right_keep, *rest = row_step(
            corners, counts, plane_index, object_tile, margin, probe, patterns, table_set, pieces
        )
        if rest:
            object_tile = rest[0]
        left_got = move(left_send, here, sharers, 1)
        cross_got = move(margin_cross, onward, sharers, 1)
        margin_got = move(margin_send, onward, sharers, 0)
        right_got = move(right_send, here, sharers, 1)
        left_pair = total(left_keep, left_got, margin_got, cross_got)
        left_far = move(left_pair, here, sharers, 2)
        right_pair = total(right_keep, right_got)
        right_far = move(right_pair, here, sharers, 2)
        left_own = total(left_pair, left_far)
        left_other = move(left_own, here, sharers, 1)
        last = repeat == ITERS - 1
        if not last:
            margin_own = move(left_own, back, sharers, 0)
            margin_other = move(left_own, back, sharers, 1)
        right_own = total(right_pair, right_far)
        right_other = move(right_own, here, sharers, 1)
        pieces = (left_own, left_other, right_own, right_other)
        if not last:
            pieces += (margin_own, margin_other)
    return finish(plane_index, object_tile, pieces)


def plain_kernel(corners, counts, extended, probe, patterns, first, second, out, *scratch):
    padded, grad = scratch
    rows = extended.shape[1]
    padded[:, :rows, :] = extended[...]
    grad[...] = jnp.zeros_like(grad)
    visit_slots(corners, counts, probe, patterns, first, second, padded, grad)
    out[...] = grad[:, :rows, :]


def plain_step(corners, counts, extended, probe, patterns, table_set):
    extent = probe.shape[1]
    rows, cols = extended.shape[1:]
    whole = pl.BlockSpec(memory_space=VMEM)
    return pl.pallas_call(
        plain_kernel,
        out_shape=jax.ShapeDtypeStruct(extended.shape, jnp.float32),
        in_specs=[pl.BlockSpec(memory_space=SMEM)] * 2 + [whole] * 5,
        out_specs=whole,
        scratch_shapes=[
            pltpu.VMEM((2, rows + SUBLANES, cols), jnp.float32),
            pltpu.VMEM((2, rows + SUBLANES, cols), jnp.float32),
        ],
        compiler_params=pltpu.CompilerParams(vmem_limit_bytes=48 << 20),
    )(corners, counts, extended, probe, patterns, *table_set)


def grid_shards(object_tile, probe, patterns, corners, counts, table_set):
    tile_count = lax.axis_size("tile")
    sharers = lax.axis_size("pos")
    grid_rows = tile_count // TILE_COLS
    extent = probe.shape[1]
    edge = object_tile.shape[1]

    def shift(value, rows, cols):
        pairs = tile_pairs(tile_count, rows, cols, grid_rows)
        return move(value.astype(jnp.bfloat16), pairs, sharers, 0).astype(jnp.float32)

    for repeat in range(ITERS):
        upper = jnp.concatenate([object_tile, shift(object_tile[:, :, :extent], 0, -1)], 2)
        lower = jnp.concatenate(
            [
                shift(object_tile[:, :extent, :], -1, 0),
                shift(object_tile[:, :extent, :extent], -1, -1),
            ],
            2,
        )
        extended = jnp.concatenate([upper, lower], 1)
        grad = plain_step(corners, counts, extended, probe, patterns, table_set)
        interior = grad[:, :edge, :edge]
        interior = interior.at[:, :, :extent].add(shift(grad[:, :edge, edge:], 0, 1))
        interior = interior.at[:, :extent, :].add(shift(grad[:, edge:, :edge], 1, 0))
        interior = interior.at[:, :extent, :extent].add(shift(grad[:, edge:, edge:], 1, 1))
        object_tile = object_tile - LEARNING_RATE * lax.psum(
            interior.astype(jnp.bfloat16), "pos"
        ).astype(jnp.float32)
    return object_tile


def shards(object_tiles, probe, patterns, corners, counts):
    table_set = tables(probe.shape[1])
    one_row = lax.axis_size("tile") == TILE_COLS
    paired = lax.axis_size("pos") == 4 and object_tiles.shape[2] == 2 * probe.shape[1]
    run = row_shards if one_row and paired else grid_shards
    return run(object_tiles[0], probe, patterns, corners, counts, table_set)[None]


def solution(mesh):
    return jax.shard_map(
        shards,
        mesh=mesh,
        in_specs=(
            P("tile", None, None, None),
            P(),
            P(("tile", "pos"), None, None),
            P(("tile", "pos"), None),
            P(("tile", "pos")),
        ),
        out_specs=P("tile", None, None, None),
        check_vma=False,
    )
```

time: 587 us -> 155 us (0.26); the launches traced: 581 us -> 155 us
  local copies, waits for them, and re-layouts: 236 us -> 8.67 us
  other arithmetic: 88.9 us -> 0.61 us
  loops' own time: 62.6 us -> 0 us
  waiting for transfers between devices: 129 us -> 85.5 us
  matrix products: 32.8 us -> 0 us
  Pallas kernels: 0 us -> 26.9 us
  starting transfers between devices: 17 us -> 32.4 us
  between operations: 14.5 us -> 0.84 us
    dynamic_update_slice x16 -> x0, local copies, waits for them, and re-layouts: 107 us -> none  [add_slot(): lax.dynamic_update_slice(running, region + slot_grads[position], anchor)]
    psum x2 -> x0, waiting for transfers between devices: 103 us -> none  [shards(): lax.psum(tile_grad.astype(jnp.bfloat16), 'pos').astype(jnp.float32)]
    gather x80 -> x0, local copies, waits for them, and re-layouts: 68.7 us -> none
    another operation x4 -> x0, loops' own time: 62.6 us -> none  [the longest x2 62.5 us: shards(): lax.fori_loop(0, slot_total, add_slot, jnp.zeros(extended.shape, jnp.floa...]
    ppermute x12 -> x19, waiting for transfers between devices: 26.4 us -> 85.5 us  [move(): return lax.ppermute(value, ('tile', 'pos'), both)]
    dynamic_slice x64 -> x0, local copies, waits for them, and re-layouts: 39.3 us -> none  [the longest x32 20.5 us: add_slot(): slot_grads[position]]
    dot_general x4 -> x0, matrix products: 32.8 us -> none  [transform(): jnp.einsum('jk,skl->sjl', left_table, halfway, preferred_element_type=jnp...]
    another operation x12 -> x0, other arithmetic: 29 us -> none
  transfers between devices with their start and end apart: 14 -> 19, of which waited for: 7 -> 16; matrix products, arithmetic and copies ran while one was open for 3% -> 1% of each run, Pallas kernels for 0% -> 0%
where the time goes in v1:
time: 155 us
  waiting for transfers between devices  85.5 us (55%)
  starting transfers between devices  32.4 us (21%)
  Pallas kernels  26.9 us (17%)
  local copies, waits for them, and re-layouts  8.67 us (6%)
    ppermute x19, waiting for transfers between devices, move(): return lax.ppermute(value, ('tile', 'pos'), both)  85.5 us
    ppermute x19, starting transfers between devices, move(): return lax.ppermute(value, ('tile', 'pos'), both)  32.4 us
    pallas_call x2, Pallas kernels, row_step(): pl.pallas_call(functools.partial(row_kernel, bool(pieces)), out_shape=out...  23.6 us
    unnamed x21, local copies, waits for them, and re-layouts  7.4 us
    pallas_call x1, Pallas kernels, finish(): pl.pallas_call(finish_kernel, out_shape=jax.ShapeDtypeStruct(tile.shape,...  3.35 us
  transfers between devices with their start and end apart: 19, of which 16 were waited for; matrix products, arithmetic and copies ran while one was open for 1% of the time, Pallas kernels for 0%

profile of v1, /device:TPU:0, one launch (start us, length us, event | category | flops | bytes accessed | tf_op | source)
XLA Modules:
  0.0 154.9 jit_solution(5632649964816403991)
XLA Ops:
  0.0 1.3 slice.7
  1.3 5.3 %collective-permute-start = (bf16[2,512,256]{2,1,0:T(8,128)(2,1)S(1)}, bf16[2,512,256]{2,1,0:T(8,128)(2,1)S(1)}, u32[]{:S(2)}, u32[]{:S(2)}) collective-permute-start(bf16[2,512,256]{2,1,0:T(8,128)(2,1)S(1)} %slice.7), channel_id=1, source_target_pairs={{0,28},{1,29},{2,30},{3,31},{4,0},{5,1},{6,2},{7,3},{8,4},{9,5},{1... | collective-permute-start | bytes 1572872 | tf_op jit(solution)/shard_map/ppermute | solution.py:249
  7.2 0.8 copy.9.corners
  8.0 5.3 %collective-permute-done.margin = bf16[2,512,256]{2,1,0:T(8,128)(2,1)S(1)} collective-permute-done((bf16[2,512,256]{2,1,0:T(8,128)(2,1)S(1)}, bf16[2,512,256]{2,1,0:T(8,128)(2,1)S(1)}, u32[]{:S(2)}, u32[]{:S(2)}) %collective-permute-start) | collective-permute-done | bytes 524320 | tf_op jit(solution)/shard_map/ppermute | solution.py:249
  13.2 1.6 %copy-done.1 = f32[1,2,512,512]{3,2,1,0:T(8,128)S(1)} copy-done((f32[1,2,512,512]{3,2,1,0:T(8,128)S(1)}, f32[1,2,512,512]{3,2,1,0:T(8,128)}, u32[]{:S(2)}) %copy-start.1) | copy-done | bytes 2097176
  14.8 1.2 copy-done.2
  16.1 1.0 copy-done.3
  17.1 1.0 copy-done.4
  18.1 1.0 copy-done.5
  19.2 11.7 %shard_map.73 = (bf16[512,256]{1,0:T(8,128)(2,1)S(1)}, f32[512,256]{1,0:T(8,128)S(1)}, bf16[512,256]{1,0:T(8,128)(2,1)S(1)}, bf16[512,256]{1,0:T(8,128)(2,1)S(1)...) custom-call(s32[8,2]{1,0:T(8,128)S(1)} %copy.9.corners, s32[1]{0:T(128)S(6)} %copy.10.counts, s32[1]{0:T(128)} %bitcast.plane_index, ...), custom_call_target="tpu_custom_call" | custom-call | flops 4294967296 | bytes 2097152 | tf_op jit(solution)/shard_map/pallas_call | solution.py:195
  30.9 0.1 collective-permute-start.1
  31.0 1.9 %collective-permute-start.2 = (bf16[512,256]{1,0:T(8,128)(2,1)S(1)}, bf16[512,256]{1,0:T(8,128)(2,1)S(1)}, u32[]{:S(2)}, u32[]{:S(2)}) collective-permute-start(bf16[512,256]{1,0:T(8,128)(2,1)S(1)} %get-tuple-element.20), channel_id=1, source_target_pairs={{0,4},{1,5},{2,6},{3,7},{4,8},{5,9},{6,10},{7,11},{8,12},{9,13},{1... | collective-permute-start | bytes 786440 | tf_op jit(solution)/shard_map/ppermute | solution.py:249
  32.9 1.9 %collective-permute-start.3 = (bf16[512,256]{1,0:T(8,128)(2,1)S(1)}, bf16[512,256]{1,0:T(8,128)(2,1)S(1)}, u32[]{:S(2)}, u32[]{:S(2)}) collective-permute-start(bf16[512,256]{1,0:T(8,128)(2,1)S(1)} %get-tuple-element.21), channel_id=1, source_target_pairs={{0,5},{1,4},{2,7},{3,6},{4,9},{5,8},{6,11},{7,10},{8,13},{9,12},{1... | collective-permute-start | bytes 786440 | tf_op jit(solution)/shard_map/ppermute | solution.py:249
  34.8 2.1 %collective-permute-start.6 = (bf16[512,256]{1,0:T(8,128)(2,1)S(1)}, bf16[512,256]{1,0:T(8,128)(2,1)S(1)}, u32[]{:S(2)}, u32[]{:S(2)}) collective-permute-start(bf16[512,256]{1,0:T(8,128)(2,1)S(1)} %get-tuple-element.23), channel_id=1, source_target_pairs={{0,1},{1,0},{2,3},{3,2},{4,5},{5,4},{6,7},{7,6},{8,9},{9,8},{10,11... | collective-permute-start | bytes 786440 | tf_op jit(solution)/shard_map/ppermute | solution.py:249
  36.9 2.3 %collective-permute-done.1 = bf16[512,256]{1,0:T(8,128)(2,1)S(1)} collective-permute-done((bf16[512,256]{1,0:T(8,128)(2,1)S(1)}, bf16[512,256]{1,0:T(8,128)(2,1)S(1)}, u32[]{:S(2)}, u32[]{:S(2)}) %collective-permute-start.1) | collective-permute-done | bytes 262176 | tf_op jit(solution)/shard_map/ppermute | solution.py:249
  39.2 0.4 collective-permute-done.2
  39.5 5.9 %collective-permute-done.3 = bf16[512,256]{1,0:T(8,128)(2,1)S(1)} collective-permute-done((bf16[512,256]{1,0:T(8,128)(2,1)S(1)}, bf16[512,256]{1,0:T(8,128)(2,1)S(1)}, u32[]{:S(2)}, u32[]{:S(2)}) %collective-permute-start.3) | collective-permute-done | bytes 262176 | tf_op jit(solution)/shard_map/ppermute | solution.py:249
  45.4 0.1 add_convert_fusion.7
  45.5 1.4 collective-permute-start.4
  47.0 1.9 %collective-permute-done.6 = bf16[512,256]{1,0:T(8,128)(2,1)S(1)} collective-permute-done((bf16[512,256]{1,0:T(8,128)(2,1)S(1)}, bf16[512,256]{1,0:T(8,128)(2,1)S(1)}, u32[]{:S(2)}, u32[]{:S(2)}) %collective-permute-start.6) | collective-permute-done | bytes 262176 | tf_op jit(solution)/shard_map/ppermute | solution.py:249
  48.9 0.1 add_convert_fusion.5
  48.9 2.9 %collective-permute-start.7 = (bf16[512,256]{1,0:T(8,128)(2,1)S(1)}, bf16[512,256]{1,0:T(8,128)(2,1)S(1)}, u32[]{:S(2)}, u32[]{:S(2)}) collective-permute-start(bf16[512,256]{1,0:T(8,128)(2,1)S(1)} %add_convert_fusion.5), channel_id=1, source_target_pairs={{0,2},{1,3},{2,0},{3,1},{4,6},{5,7},{6,4},{7,5},{8,10},{9,11},{10,... | collective-permute-start | bytes 786440 | tf_op jit(solution)/shard_map/ppermute | solution.py:249
  51.9 14.9 %collective-permute-done.4 = bf16[512,256]{1,0:T(8,128)(2,1)S(1)} collective-permute-done((bf16[512,256]{1,0:T(8,128)(2,1)S(1)}, bf16[512,256]{1,0:T(8,128)(2,1)S(1)}, u32[]{:S(2)}, u32[]{:S(2)}) %collective-permute-start.4) | collective-permute-done | bytes 262176 | tf_op jit(solution)/shard_map/ppermute | solution.py:249
  66.8 0.1 add_convert_fusion.6.rest_0_
  66.9 1.9 %collective-permute-start.10 = (bf16[512,256]{1,0:T(8,128)(2,1)S(1)}, bf16[512,256]{1,0:T(8,128)(2,1)S(1)}, u32[]{:S(2)}, u32[]{:S(2)}) collective-permute-start(bf16[512,256]{1,0:T(8,128)(2,1)S(1)} %add_convert_fusion.6.rest_0_), channel_id=1, source_target_pairs={{0,29},{1,28},{2,31},{3,30},{4,1},{5,0},{6,3},{7,2},{8,5},{9,4},{1... | collective-permute-start | bytes 786440 | tf_op jit(solution)/shard_map/ppermute | solution.py:249
  68.8 3.1 %collective-permute-start.9 = (bf16[512,256]{1,0:T(8,128)(2,1)S(1)}, bf16[512,256]{1,0:T(8,128)(2,1)S(1)}, u32[]{:S(2)}, u32[]{:S(2)}) collective-permute-start(bf16[512,256]{1,0:T(8,128)(2,1)S(1)} %add_convert_fusion.6.rest_0_), channel_id=1, source_target_pairs={{0,28},{1,29},{2,30},{3,31},{4,0},{5,1},{6,2},{7,3},{8,4},{9,5},{1... | collective-permute-start | bytes 786440 | tf_op jit(solution)/shard_map/ppermute | solution.py:249
  71.9 2.2 %collective-permute-start.5 = (bf16[512,256]{1,0:T(8,128)(2,1)S(1)}, bf16[512,256]{1,0:T(8,128)(2,1)S(1)}, u32[]{:S(2)}, u32[]{:S(2)}) collective-permute-start(bf16[512,256]{1,0:T(8,128)(2,1)S(1)} %add_convert_fusion.6.rest_0_), channel_id=1, source_target_pairs={{0,1},{1,0},{2,3},{3,2},{4,5},{5,4},{6,7},{7,6},{8,9},{9,8},{10,11... | collective-permute-start | bytes 786440 | tf_op jit(solution)/shard_map/ppermute | solution.py:249
  74.1 0.0 collective-permute-done.7
  74.1 0.1 add_convert_fusion.4.rest_2_
  74.2 0.1 collective-permute-start.8
  74.3 3.1 %collective-permute-done.10.rest_5_ = bf16[512,256]{1,0:T(8,128)(2,1)S(1)} collective-permute-done((bf16[512,256]{1,0:T(8,128)(2,1)S(1)}, bf16[512,256]{1,0:T(8,128)(2,1)S(1)}, u32[]{:S(2)}, u32[]{:S(2)}) %collective-permute-start.10) | collective-permute-done | bytes 262176 | tf_op jit(solution)/shard_map/ppermute | solution.py:249
  77.4 0.0 collective-permute-done.9.rest_4_
  77.4 4.2 %collective-permute-done.5.rest_1_ = bf16[512,256]{1,0:T(8,128)(2,1)S(1)} collective-permute-done((bf16[512,256]{1,0:T(8,128)(2,1)S(1)}, bf16[512,256]{1,0:T(8,128)(2,1)S(1)}, u32[]{:S(2)}, u32[]{:S(2)}) %collective-permute-start.5) | collective-permute-done | bytes 262176 | tf_op jit(solution)/shard_map/ppermute | solution.py:249
  81.6 5.6 %collective-permute-done.8.rest_3_ = bf16[512,256]{1,0:T(8,128)(2,1)S(1)} collective-permute-done((bf16[512,256]{1,0:T(8,128)(2,1)S(1)}, bf16[512,256]{1,0:T(8,128)(2,1)S(1)}, u32[]{:S(2)}, u32[]{:S(2)}) %collective-permute-start.8) | collective-permute-done | bytes 262176 | tf_op jit(solution)/shard_map/ppermute | solution.py:249
  87.2 11.9 %shard_map.74 = (bf16[512,256]{1,0:T(8,128)(2,1)S(1)}, f32[512,256]{1,0:T(8,128)S(1)}, bf16[512,256]{1,0:T(8,128)(2,1)S(1)}, bf16[512,256]{1,0:T(8,128)(2,1)S(1)...) custom-call(s32[8,2]{1,0:T(8,128)S(1)} %copy.9.corners, s32[1]{0:T(128)S(6)} %copy.10.counts, ...), custom_call_target="tpu_custom_call" | custom-call | flops 4294967296 | bytes 2097152 | tf_op jit(solution)/shard_map/pallas_call | solution.py:195
  99.1 0.0 copy-start
  99.1 0.1 collective-permute-start.11
  99.2 1.9 %collective-permute-start.12 = (bf16[512,256]{1,0:T(8,128)(2,1)S(1)}, bf16[512,256]{1,0:T(8,128)(2,1)S(1)}, u32[]{:S(2)}, u32[]{:S(2)}) collective-permute-start(bf16[512,256]{1,0:T(8,128)(2,1)S(1)} %get-tuple-element.27), channel_id=1, source_target_pairs={{0,4},{1,5},{2,6},{3,7},{4,8},{5,9},{6,10},{7,11},{8,12},{9,13},{1... | collective-permute-start | bytes 786440 | tf_op jit(solution)/shard_map/ppermute | solution.py:249
  101.1 1.9 %collective-permute-start.13 = (bf16[512,256]{1,0:T(8,128)(2,1)S(1)}, bf16[512,256]{1,0:T(8,128)(2,1)S(1)}, u32[]{:S(2)}, u32[]{:S(2)}) collective-permute-start(bf16[512,256]{1,0:T(8,128)(2,1)S(1)} %get-tuple-element.28), channel_id=1, source_target_pairs={{0,5},{1,4},{2,7},{3,6},{4,9},{5,8},{6,11},{7,10},{8,13},{9,12},{1... | collective-permute-start | bytes 786440 | tf_op jit(solution)/shard_map/ppermute | solution.py:249
  103.0 2.1 %collective-permute-start.16 = (bf16[512,256]{1,0:T(8,128)(2,1)S(1)}, bf16[512,256]{1,0:T(8,128)(2,1)S(1)}, u32[]{:S(2)}, u32[]{:S(2)}) collective-permute-start(bf16[512,256]{1,0:T(8,128)(2,1)S(1)} %get-tuple-element.30), channel_id=1, source_target_pairs={{0,1},{1,0},{2,3},{3,2},{4,5},{5,4},{6,7},{7,6},{8,9},{9,8},{10,11... | collective-permute-start | bytes 786440 | tf_op jit(solution)/shard_map/ppermute | solution.py:249
  105.1 3.2 %collective-permute-done.11 = bf16[512,256]{1,0:T(8,128)(2,1)S(1)} collective-permute-done((bf16[512,256]{1,0:T(8,128)(2,1)S(1)}, bf16[512,256]{1,0:T(8,128)(2,1)S(1)}, u32[]{:S(2)}, u32[]{:S(2)}) %collective-permute-start.11) | collective-permute-done | bytes 262176 | tf_op jit(solution)/shard_map/ppermute | solution.py:249
  108.3 0.0 collective-permute-done.12
  108.3 5.3 %collective-permute-done.13 = bf16[512,256]{1,0:T(8,128)(2,1)S(1)} collective-permute-done((bf16[512,256]{1,0:T(8,128)(2,1)S(1)}, bf16[512,256]{1,0:T(8,128)(2,1)S(1)}, u32[]{:S(2)}, u32[]{:S(2)}) %collective-permute-start.13) | collective-permute-done | bytes 262176 | tf_op jit(solution)/shard_map/ppermute | solution.py:249
  113.6 0.1 add_convert_fusion.3
  113.8 1.2 collective-permute-start.14
  114.9 1.8 %collective-permute-done.16 = bf16[512,256]{1,0:T(8,128)(2,1)S(1)} collective-permute-done((bf16[512,256]{1,0:T(8,128)(2,1)S(1)}, bf16[512,256]{1,0:T(8,128)(2,1)S(1)}, u32[]{:S(2)}, u32[]{:S(2)}) %collective-permute-start.16) | collective-permute-done | bytes 262176 | tf_op jit(solution)/shard_map/ppermute | solution.py:249
  116.8 0.1 add_convert_fusion.1
  116.8 2.1 %collective-permute-start.17 = (bf16[512,256]{1,0:T(8,128)(2,1)S(1)}, bf16[512,256]{1,0:T(8,128)(2,1)S(1)}, u32[]{:S(2)}, u32[]{:S(2)}) collective-permute-start(bf16[512,256]{1,0:T(8,128)(2,1)S(1)} %add_convert_fusion.1), channel_id=1, source_target_pairs={{0,2},{1,3},{2,0},{3,1},{4,6},{5,7},{6,4},{7,5},{8,10},{9,11},{10,... | collective-permute-start | bytes 786440 | tf_op jit(solution)/shard_map/ppermute | solution.py:249
  119.0 15.5 %collective-permute-done.14 = bf16[512,256]{1,0:T(8,128)(2,1)S(1)} collective-permute-done((bf16[512,256]{1,0:T(8,128)(2,1)S(1)}, bf16[512,256]{1,0:T(8,128)(2,1)S(1)}, u32[]{:S(2)}, u32[]{:S(2)}) %collective-permute-start.14) | collective-permute-done | bytes 262176 | tf_op jit(solution)/shard_map/ppermute | solution.py:249
  134.5 0.1 add_convert_fusion.2.left_own
  134.5 0.0 copy-start.6
  134.5 0.1 collective-permute-start.15
  134.6 5.1 %collective-permute-done.17 = bf16[512,256]{1,0:T(8,128)(2,1)S(1)} collective-permute-done((bf16[512,256]{1,0:T(8,128)(2,1)S(1)}, bf16[512,256]{1,0:T(8,128)(2,1)S(1)}, u32[]{:S(2)}, u32[]{:S(2)}) %collective-permute-start.17) | collective-permute-done | bytes 262176 | tf_op jit(solution)/shard_map/ppermute | solution.py:249
  139.8 0.1 add_convert_fusion.right_own
  139.8 0.0 copy-done
  139.8 0.0 copy-start.7
  139.9 0.1 collective-permute-start.18
  139.9 5.4 %collective-permute-done.15.left_other = bf16[512,256]{1,0:T(8,128)(2,1)S(1)} collective-permute-done((bf16[512,256]{1,0:T(8,128)(2,1)S(1)}, bf16[512,256]{1,0:T(8,128)(2,1)S(1)}, u32[]{:S(2)}, u32[]{:S(2)}) %collective-permute-start.15) | collective-permute-done | bytes 262176 | tf_op jit(solution)/shard_map/ppermute | solution.py:249
  145.4 5.5 %collective-permute-done.18.right_other = bf16[512,256]{1,0:T(8,128)(2,1)S(1)} collective-permute-done((bf16[512,256]{1,0:T(8,128)(2,1)S(1)}, bf16[512,256]{1,0:T(8,128)(2,1)S(1)}, u32[]{:S(2)}, u32[]{:S(2)}) %collective-permute-start.18) | collective-permute-done | bytes 262176 | tf_op jit(solution)/shard_map/ppermute | solution.py:249
  150.9 0.0 copy-done.6
  150.9 0.0 copy-done.7
  150.9 0.0 copy-done.8
  150.9 0.7 copy-done.9
  151.6 3.3 %shard_map.75 = f32[2,512,512]{2,1,0:T(8,128)} custom-call(s32[1]{0:T(128)} %bitcast.plane_index, f32[2,512,512]{2,1,0:T(8,128)} %copy-done, bf16[512,256]{1,0:T(8,128)(2,1)} %copy-done.6, bf16[512,256]{1,0:T(8,128)(2,1)} %copy-done.8, bf16[512,256]{1,0:T(8,128)(2,1)} %copy-done.7, bf16[512,256]{1,0:T(8,128)(2,1)} %copy-done.9), custom_call_target="tpu_custom_call" | custom-call | tf_op jit(solution)/shard_map/pallas_call | solution.py:223
  (7 shorter events, 0.0 us)
Async XLA Ops:
  1.3 12.0 %collective-permute-start = (bf16[2,512,256]{2,1,0:T(8,128)(2,1)S(1)}, bf16[2,512,256]{2,1,0:T(8,128)(2,1)S(1)}, u32[]{:S(2)}, u32[]{:S(2)}) collective-permute-start(bf16[2,512,256]{2,1,0:T(8,128)(2,1)S(1)} %slice.7), channel_id=1, source_target_pairs={{0,28},{1,29},{2,30},{3,31},{4,0},{5,1},{6,2},{7,3},{8,4},{9,5},{1... | collective-permute-start | bytes 1572872 | tf_op jit(solution)/shard_map/ppermute | solution.py:249
  13.2 1.6 %copy-start.1 = (f32[1,2,512,512]{3,2,1,0:T(8,128)S(1)}, f32[1,2,512,512]{3,2,1,0:T(8,128)}, u32[]{:S(2)}) copy-start(f32[1,2,512,512]{3,2,1,0:T(8,128)} %param.7) | copy-start | bytes 6291460
  14.8 1.2 copy-start.2
  16.1 1.0 copy-start.3
  17.1 1.0 copy-start.4
  18.1 1.0 copy-start.5
  30.9 8.3 %collective-permute-start.1 = (bf16[512,256]{1,0:T(8,128)(2,1)S(1)}, bf16[512,256]{1,0:T(8,128)(2,1)S(1)}, u32[]{:S(2)}, u32[]{:S(2)}) collective-permute-start(bf16[512,256]{1,0:T(8,128)(2,1)S(1)} %get-tuple-element.19), channel_id=1, source_target_pairs={{0,1},{1,0},{2,3},{3,2},{4,5},{5,4},{6,7},{7,6},{8,9},{9,8},{10,11... | collective-permute-start | bytes 786440 | tf_op jit(solution)/shard_map/ppermute | solution.py:249
  31.0 8.6 %collective-permute-start.2 = (bf16[512,256]{1,0:T(8,128)(2,1)S(1)}, bf16[512,256]{1,0:T(8,128)(2,1)S(1)}, u32[]{:S(2)}, u32[]{:S(2)}) collective-permute-start(bf16[512,256]{1,0:T(8,128)(2,1)S(1)} %get-tuple-element.20), channel_id=1, source_target_pairs={{0,4},{1,5},{2,6},{3,7},{4,8},{5,9},{6,10},{7,11},{8,12},{9,13},{1... | collective-permute-start | bytes 786440 | tf_op jit(solution)/shard_map/ppermute | solution.py:249
  32.9 12.5 %collective-permute-start.3 = (bf16[512,256]{1,0:T(8,128)(2,1)S(1)}, bf16[512,256]{1,0:T(8,128)(2,1)S(1)}, u32[]{:S(2)}, u32[]{:S(2)}) collective-permute-start(bf16[512,256]{1,0:T(8,128)(2,1)S(1)} %get-tuple-element.21), channel_id=1, source_target_pairs={{0,5},{1,4},{2,7},{3,6},{4,9},{5,8},{6,11},{7,10},{8,13},{9,12},{1... | collective-permute-start | bytes 786440 | tf_op jit(solution)/shard_map/ppermute | solution.py:249
  34.8 14.1 %collective-permute-start.6 = (bf16[512,256]{1,0:T(8,128)(2,1)S(1)}, bf16[512,256]{1,0:T(8,128)(2,1)S(1)}, u32[]{:S(2)}, u32[]{:S(2)}) collective-permute-start(bf16[512,256]{1,0:T(8,128)(2,1)S(1)} %get-tuple-element.23), channel_id=1, source_target_pairs={{0,1},{1,0},{2,3},{3,2},{4,5},{5,4},{6,7},{7,6},{8,9},{9,8},{10,11... | collective-permute-start | bytes 786440 | tf_op jit(solution)/shard_map/ppermute | solution.py:249
  45.5 21.3 %collective-permute-start.4 = (bf16[512,256]{1,0:T(8,128)(2,1)S(1)}, bf16[512,256]{1,0:T(8,128)(2,1)S(1)}, u32[]{:S(2)}, u32[]{:S(2)}) collective-permute-start(bf16[512,256]{1,0:T(8,128)(2,1)S(1)} %add_convert_fusion.7), channel_id=1, source_target_pairs={{0,2},{1,3},{2,0},{3,1},{4,6},{5,7},{6,4},{7,5},{8,10},{9,11},{10,... | collective-permute-start | bytes 786440 | tf_op jit(solution)/shard_map/ppermute | solution.py:249
  48.9 25.2 %collective-permute-start.7 = (bf16[512,256]{1,0:T(8,128)(2,1)S(1)}, bf16[512,256]{1,0:T(8,128)(2,1)S(1)}, u32[]{:S(2)}, u32[]{:S(2)}) collective-permute-start(bf16[512,256]{1,0:T(8,128)(2,1)S(1)} %add_convert_fusion.5), channel_id=1, source_target_pairs={{0,2},{1,3},{2,0},{3,1},{4,6},{5,7},{6,4},{7,5},{8,10},{9,11},{10,... | collective-permute-start | bytes 786440 | tf_op jit(solution)/shard_map/ppermute | solution.py:249
  66.9 10.5 %collective-permute-start.10 = (bf16[512,256]{1,0:T(8,128)(2,1)S(1)}, bf16[512,256]{1,0:T(8,128)(2,1)S(1)}, u32[]{:S(2)}, u32[]{:S(2)}) collective-permute-start(bf16[512,256]{1,0:T(8,128)(2,1)S(1)} %add_convert_fusion.6.rest_0_), channel_id=1, source_target_pairs={{0,29},{1,28},{2,31},{3,30},{4,1},{5,0},{6,3},{7,2},{8,5},{9,4},{1... | collective-permute-start | bytes 786440 | tf_op jit(solution)/shard_map/ppermute | solution.py:249
  68.8 8.6 %collective-permute-start.9 = (bf16[512,256]{1,0:T(8,128)(2,1)S(1)}, bf16[512,256]{1,0:T(8,128)(2,1)S(1)}, u32[]{:S(2)}, u32[]{:S(2)}) collective-permute-start(bf16[512,256]{1,0:T(8,128)(2,1)S(1)} %add_convert_fusion.6.rest_0_), channel_id=1, source_target_pairs={{0,28},{1,29},{2,30},{3,31},{4,0},{5,1},{6,2},{7,3},{8,4},{9,5},{1... | collective-permute-start | bytes 786440 | tf_op jit(solution)/shard_map/ppermute | solution.py:249
  71.9 9.7 %collective-permute-start.5 = (bf16[512,256]{1,0:T(8,128)(2,1)S(1)}, bf16[512,256]{1,0:T(8,128)(2,1)S(1)}, u32[]{:S(2)}, u32[]{:S(2)}) collective-permute-start(bf16[512,256]{1,0:T(8,128)(2,1)S(1)} %add_convert_fusion.6.rest_0_), channel_id=1, source_target_pairs={{0,1},{1,0},{2,3},{3,2},{4,5},{5,4},{6,7},{7,6},{8,9},{9,8},{10,11... | collective-permute-start | bytes 786440 | tf_op jit(solution)/shard_map/ppermute | solution.py:249
  74.2 13.0 %collective-permute-start.8 = (bf16[512,256]{1,0:T(8,128)(2,1)S(1)}, bf16[512,256]{1,0:T(8,128)(2,1)S(1)}, u32[]{:S(2)}, u32[]{:S(2)}) collective-permute-start(bf16[512,256]{1,0:T(8,128)(2,1)S(1)} %add_convert_fusion.4.rest_2_), channel_id=1, source_target_pairs={{0,1},{1,0},{2,3},{3,2},{4,5},{5,4},{6,7},{7,6},{8,9},{9,8},{10,11... | collective-permute-start | bytes 786440 | tf_op jit(solution)/shard_map/ppermute | solution.py:249
  99.1 40.7 %copy-start = (f32[2,512,512]{2,1,0:T(8,128)}, f32[2,512,512]{2,1,0:T(8,128)S(1)}, u32[]{:S(2)}) copy-start(f32[2,512,512]{2,1,0:T(8,128)S(1)} %get-tuple-element.24.tile) | copy-start | bytes 6291460
  99.1 9.2 %collective-permute-start.11 = (bf16[512,256]{1,0:T(8,128)(2,1)S(1)}, bf16[512,256]{1,0:T(8,128)(2,1)S(1)}, u32[]{:S(2)}, u32[]{:S(2)}) collective-permute-start(bf16[512,256]{1,0:T(8,128)(2,1)S(1)} %get-tuple-element.26), channel_id=1, source_target_pairs={{0,1},{1,0},{2,3},{3,2},{4,5},{5,4},{6,7},{7,6},{8,9},{9,8},{10,11... | collective-permute-start | bytes 786440 | tf_op jit(solution)/shard_map/ppermute | solution.py:249
  99.2 9.2 %collective-permute-start.12 = (bf16[512,256]{1,0:T(8,128)(2,1)S(1)}, bf16[512,256]{1,0:T(8,128)(2,1)S(1)}, u32[]{:S(2)}, u32[]{:S(2)}) collective-permute-start(bf16[512,256]{1,0:T(8,128)(2,1)S(1)} %get-tuple-element.27), channel_id=1, source_target_pairs={{0,4},{1,5},{2,6},{3,7},{4,8},{5,9},{6,10},{7,11},{8,12},{9,13},{1... | collective-permute-start | bytes 786440 | tf_op jit(solution)/shard_map/ppermute | solution.py:249
  101.1 12.5 %collective-permute-start.13 = (bf16[512,256]{1,0:T(8,128)(2,1)S(1)}, bf16[512,256]{1,0:T(8,128)(2,1)S(1)}, u32[]{:S(2)}, u32[]{:S(2)}) collective-permute-start(bf16[512,256]{1,0:T(8,128)(2,1)S(1)} %get-tuple-element.28), channel_id=1, source_target_pairs={{0,5},{1,4},{2,7},{3,6},{4,9},{5,8},{6,11},{7,10},{8,13},{9,12},{1... | collective-permute-start | bytes 786440 | tf_op jit(solution)/shard_map/ppermute | solution.py:249
  103.0 13.7 %collective-permute-start.16 = (bf16[512,256]{1,0:T(8,128)(2,1)S(1)}, bf16[512,256]{1,0:T(8,128)(2,1)S(1)}, u32[]{:S(2)}, u32[]{:S(2)}) collective-permute-start(bf16[512,256]{1,0:T(8,128)(2,1)S(1)} %get-tuple-element.30), channel_id=1, source_target_pairs={{0,1},{1,0},{2,3},{3,2},{4,5},{5,4},{6,7},{7,6},{8,9},{9,8},{10,11... | collective-permute-start | bytes 786440 | tf_op jit(solution)/shard_map/ppermute | solution.py:249
  113.8 20.7 %collective-permute-start.14 = (bf16[512,256]{1,0:T(8,128)(2,1)S(1)}, bf16[512,256]{1,0:T(8,128)(2,1)S(1)}, u32[]{:S(2)}, u32[]{:S(2)}) collective-permute-start(bf16[512,256]{1,0:T(8,128)(2,1)S(1)} %add_convert_fusion.3), channel_id=1, source_target_pairs={{0,2},{1,3},{2,0},{3,1},{4,6},{5,7},{6,4},{7,5},{8,10},{9,11},{10,... | collective-permute-start | bytes 786440 | tf_op jit(solution)/shard_map/ppermute | solution.py:249
  116.8 22.9 %collective-permute-start.17 = (bf16[512,256]{1,0:T(8,128)(2,1)S(1)}, bf16[512,256]{1,0:T(8,128)(2,1)S(1)}, u32[]{:S(2)}, u32[]{:S(2)}) collective-permute-start(bf16[512,256]{1,0:T(8,128)(2,1)S(1)} %add_convert_fusion.1), channel_id=1, source_target_pairs={{0,2},{1,3},{2,0},{3,1},{4,6},{5,7},{6,4},{7,5},{8,10},{9,11},{10,... | collective-permute-start | bytes 786440 | tf_op jit(solution)/shard_map/ppermute | solution.py:249
  134.5 16.4 %copy-start.6 = (bf16[512,256]{1,0:T(8,128)(2,1)}, bf16[512,256]{1,0:T(8,128)(2,1)S(1)}, u32[]{:S(2)}) copy-start(bf16[512,256]{1,0:T(8,128)(2,1)S(1)} %add_convert_fusion.2.left_own) | copy-start | bytes 786436
  134.5 10.8 %collective-permute-start.15 = (bf16[512,256]{1,0:T(8,128)(2,1)S(1)}, bf16[512,256]{1,0:T(8,128)(2,1)S(1)}, u32[]{:S(2)}, u32[]{:S(2)}) collective-permute-start(bf16[512,256]{1,0:T(8,128)(2,1)S(1)} %add_convert_fusion.2.left_own), channel_id=1, source_target_pairs={{0,1},{1,0},{2,3},{3,2},{4,5},{5,4},{6,7},{7,6},{8,9},{9,8},{10,11... | collective-permute-start | bytes 786440 | tf_op jit(solution)/shard_map/ppermute | solution.py:249
  139.8 11.1 %copy-start.7 = (bf16[512,256]{1,0:T(8,128)(2,1)}, bf16[512,256]{1,0:T(8,128)(2,1)S(1)}, u32[]{:S(2)}) copy-start(bf16[512,256]{1,0:T(8,128)(2,1)S(1)} %add_convert_fusion.right_own) | copy-start | bytes 786436
  139.9 11.0 %collective-permute-start.18 = (bf16[512,256]{1,0:T(8,128)(2,1)S(1)}, bf16[512,256]{1,0:T(8,128)(2,1)S(1)}, u32[]{:S(2)}, u32[]{:S(2)}) collective-permute-start(bf16[512,256]{1,0:T(8,128)(2,1)S(1)} %add_convert_fusion.right_own), channel_id=1, source_target_pairs={{0,1},{1,0},{2,3},{3,2},{4,5},{5,4},{6,7},{7,6},{8,9},{9,8},{10,11... | collective-permute-start | bytes 786440 | tf_op jit(solution)/shard_map/ppermute | solution.py:249
  145.4 5.5 %copy-start.8 = (bf16[512,256]{1,0:T(8,128)(2,1)}, bf16[512,256]{1,0:T(8,128)(2,1)S(1)}, u32[]{:S(2)}) copy-start(bf16[512,256]{1,0:T(8,128)(2,1)S(1)} %collective-permute-done.15.left_other) | copy-start | bytes 786436
  150.9 0.7 copy-start.9

commit v2 on v1

--- a/solution.py
+++ b/solution.py
@@ -14,8 +14,10 @@
 LEARNING_RATE = 0.03
 LANES = 128
 SUBLANES = 8
+LIMIT = 24 << 20
 VMEM = pltpu.VMEM
 SMEM = pltpu.SMEM
+HBM = pltpu.MemorySpace.HBM
 
 
 def tables(extent):
@@ -42,12 +44,12 @@
     return jnp.dot(left_table, stacked, preferred_element_type=jnp.float32)
 
 
-def visit_slots(corners, counts, probe, patterns, first, second, extended, grad):
+def visit_slots(chosen, corners, counts, probe, patterns, first, second, extended, grad):
     extent = patterns.shape[1]
     rows_iota = lax.broadcasted_iota(jnp.int32, (SUBLANES, LANES), 0)
     lane_iota = lax.broadcasted_iota(jnp.int32, (extent, LANES), 1)
 
-    def visit(slot, carry):
+    def visit(slot):
         row_at = corners[slot, 0]
         col_at = corners[slot, 1]
         row_base = pl.multiple_of(row_at // SUBLANES * SUBLANES, SUBLANES)
@@ -114,118 +116,161 @@
 
         add_window(0, probe_re * grad_re + probe_im * grad_im)
         add_window(1, probe_re * grad_im - probe_im * grad_re)
+
+    def step(slot, carry):
+        pl.when(chosen(corners[slot, 1]))(functools.partial(visit, slot))
         return carry
 
-    lax.fori_loop(0, counts[0], visit, 0)
-
-
-def row_kernel(
-    with_update,
-    corners,
-    counts,
-    plane_index,
-    tile,
-    margin,
-    probe,
-    patterns,
-    first,
-    second,
-    *rest,
-):
-    if with_update:
-        left_own, left_other, right_own, right_other, margin_own, margin_other, *rest = rest
-    (
-        left_send,
-        left_keep,
-        margin_send,
-        margin_cross,
-        right_send,
-        right_keep,
-        *rest,
-    ) = rest
-    if with_update:
-        tile_out, *rest = rest
-    extended, grad = rest
+    lax.fori_loop(0, counts[0], step, 0)
+
+
+def block_of(index, extent):
+    return (
+        slice(index % 2 * extent, (index % 2 + 1) * extent),
+        slice(index // 2 * extent, (index // 2 + 1) * extent),
+    )
+
+
+def take_step(extended, pieces, own, first_index):
+    extent = pieces[0].shape[1]
+    count = len(pieces) // 2
+    for index, piece in enumerate(pieces):
+        plane = own if index < count else 1 - own
+        rows, cols = block_of(first_index + index % count, extent)
+        extended[plane, rows, cols] -= LEARNING_RATE * piece[...].astype(jnp.float32)
+
+
+def load_kernel(edge, corners, counts, tile, *rest):
+    loads, (extended, grad, *held), sems = rest[:4], rest[4:10], rest[10]
+    copies = [
+        pltpu.make_async_copy(source, target, sems.at[index])
+        for index, (source, target) in enumerate(
+            zip((tile, *loads), (extended.at[:, :edge, :edge], *held))
+        )
+    ]
+    for copy in copies:
+        copy.start()
+    grad[...] = jnp.zeros_like(grad)
+    for copy in copies:
+        copy.wait()
+    extent = held[0].shape[1]
+    visit_slots(lambda col: col + extent <= edge, corners, counts, *held, extended, grad)
+
+
+def inner_kernel(edge, corners, counts, plane_index, *rest):
+    held, pieces, (extended, grad) = rest[:4], rest[6:14], rest[14:]
+    grad[...] = jnp.zeros_like(grad)
+    take_step(extended, pieces, plane_index[0], 0)
+    extent = held[0].shape[1]
+    visit_slots(lambda col: col + extent <= edge, corners, counts, *held, extended, grad)
+
+
+def outer_kernel(edge, corners, counts, plane_index, *rest):
+    held, rest = rest[:4], rest[6:]
+    margins, (extended, grad, margin_send, *halves) = rest[:-11], rest[-11:]
+    extent = held[0].shape[1]
+    own = plane_index[0]
+    other = 1 - own
+    beyond = slice(edge, edge + extent)
+    if len(margins) == 1:
+        for plane in (0, 1):
+            extended[plane, :edge, beyond] = margins[0][plane].astype(jnp.float32)
+    else:
+        take_step(extended, margins, own, 4)
+    visit_slots(lambda col: col + extent > edge, corners, counts, *held, extended, grad)
+    margin_send[0] = grad[own, :edge, beyond].astype(jnp.bfloat16)
+    margin_send[1] = grad[other, :edge, beyond].astype(jnp.bfloat16)
+    for index, half in enumerate(halves):
+        rows, cols = block_of(index // 4 * 2 + index % 2, extent)
+        plane = (own, other)[index % 4 // 2]
+        half[...] = grad[plane, rows, cols].astype(half.dtype)
+
+
+WHOLE = pl.BlockSpec(memory_space=VMEM)
+SCALAR = pl.BlockSpec(memory_space=SMEM)
+
+
+def slot_cost(extent, slots):
+    return pl.CostEstimate(
+        flops=slots * 16 * extent**3, bytes_accessed=64 * extent * extent, transcendentals=0
+    )
+
+
+def load_step(corners, counts, tile, probe, patterns, table_set):
     extent = probe.shape[1]
     edge = tile.shape[1]
+    loads = (probe, patterns, *table_set)
+    image = jax.ShapeDtypeStruct((2, edge + SUBLANES, edge + extent), jnp.float32)
+    extended, grad, *held = pl.pallas_call(
+        functools.partial(load_kernel, edge),
+        out_shape=[image, image] + [jax.ShapeDtypeStruct(v.shape, v.dtype) for v in loads],
+        in_specs=[SCALAR] * 2 + [pl.BlockSpec(memory_space=HBM)] * 5,
+        out_specs=[WHOLE] * 6,
+        scratch_shapes=[pltpu.SemaphoreType.DMA((5,))],
+        cost_estimate=slot_cost(extent, patterns.shape[0]),
+        compiler_params=pltpu.CompilerParams(vmem_limit_bytes=LIMIT),
+    )(corners, counts, *(pltpu.with_memory_space_constraint(v, HBM) for v in (tile, *loads)))
+    return extended, grad, held
+
+
+def inner_step(corners, counts, plane_index, held, extended, grad, edge, pieces):
+    return pl.pallas_call(
+        functools.partial(inner_kernel, edge),
+        out_shape=[jax.ShapeDtypeStruct(v.shape, v.dtype) for v in (extended, grad)],
+        in_specs=[SCALAR] * 3 + [WHOLE] * (6 + len(pieces)),
+        out_specs=[WHOLE] * 2,
+        input_output_aliases={7: 0, 8: 1},
+        cost_estimate=slot_cost(held[0].shape[1], held[1].shape[0]),
+        compiler_params=pltpu.CompilerParams(vmem_limit_bytes=LIMIT),
+    )(corners, counts, plane_index, *held, extended, grad, *pieces)
+
+
+def outer_step(corners, counts, plane_index, held, extended, grad, edge, margins):
+    extent = held[0].shape[1]
+    half = jax.ShapeDtypeStruct((extent, extent), jnp.bfloat16)
+    wide = jax.ShapeDtypeStruct((extent, extent), jnp.float32)
+    outs = [jax.ShapeDtypeStruct(v.shape, v.dtype) for v in (extended, grad)]
+    outs.append(jax.ShapeDtypeStruct((2, edge, extent), jnp.bfloat16))
+    outs += [wide] * 6 + [half] * 2
+    extended, grad, margin_send, *halves = pl.pallas_call(
+        functools.partial(outer_kernel, edge),
+        out_shape=outs,
+        in_specs=[SCALAR] * 3 + [WHOLE] * (6 + len(margins)),
+        out_specs=[WHOLE] * len(outs),
+        input_output_aliases={7: 0, 8: 1},
+        cost_estimate=slot_cost(extent, held[1].shape[0]),
+        compiler_params=pltpu.CompilerParams(vmem_limit_bytes=LIMIT),
+    )(corners, counts, plane_index, *held, extended, grad, *margins)
+    return extended, grad, margin_send, halves
+
+
+def finish_kernel(block, plane_index, extended, own_top, own_low, other_top, other_low, *rest):
+    out = rest[-1]
     own = plane_index[0]
-    other = 1 - own
-    if with_update:
-        for plane, pieces in (
-            (own, (left_own, right_own, margin_own)),
-            (other, (left_other, right_other, margin_other)),
-        ):
-            for block, piece in enumerate(pieces):
-                step = LEARNING_RATE * piece[...].astype(jnp.float32)
-                cols = slice(block * extent, (block + 1) * extent)
-                if block * extent < edge:
-                    value = tile[plane, :, cols] - step
-                    tile_out[plane, :, cols] = value
-                else:
-                    value = margin[plane].astype(jnp.float32) - step
-                extended[plane, :edge, cols] = value
-    else:
-        for plane in (0, 1):
-            extended[plane, :edge, :edge] = tile[plane]
-            extended[plane, :edge, edge:] = margin[plane].astype(jnp.float32)
-    grad[...] = jnp.zeros_like(grad)
-    visit_slots(corners, counts, probe, patterns, first, second, extended, grad)
-    left = slice(0, extent)
-    right = slice(extent, edge)
-    beyond = slice(edge, edge + extent)
-    left_send[...] = grad[other, :edge, left].astype(jnp.bfloat16)
-    left_keep[...] = grad[own, :edge, left]
-    margin_send[...] = grad[own, :edge, beyond].astype(jnp.bfloat16)
-    margin_cross[...] = grad[other, :edge, beyond].astype(jnp.bfloat16)
-    right_send[...] = grad[other, :edge, right].astype(jnp.bfloat16)
-    right_keep[...] = grad[own, :edge, right]
-
-
-def row_step(corners, counts, plane_index, tile, margin, probe, patterns, table_set, pieces):
-    extent = probe.shape[1]
-    edge = tile.shape[1]
-    slots = patterns.shape[0]
-    half = jax.ShapeDtypeStruct((edge, extent), jnp.bfloat16)
-    wide = jax.ShapeDtypeStruct((edge, extent), jnp.float32)
-    outs = [half, wide, half, half, half, wide]
-    if pieces:
-        outs.append(jax.ShapeDtypeStruct(tile.shape, jnp.float32))
-    whole = pl.BlockSpec(memory_space=VMEM)
-    scalar = pl.BlockSpec(memory_space=SMEM)
+    extent = own_top.shape[0]
+    for plane, pieces in ((own, (own_top, own_low)), (1 - own, (other_top, other_low))):
+        for half, piece in enumerate(pieces):
+            rows, cols = block_of(2 * block + half, extent)
+            step = LEARNING_RATE * piece[...].astype(jnp.float32)
+            out[plane, rows] = extended[plane, rows, cols] - step
+
+
+def finish(plane_index, extended, edge, pieces, block, partial):
+    extent = pieces[0].shape[1]
+    column = pl.BlockSpec((2, edge, extent), lambda step: (0, 0, block))
+    earlier = [] if partial is None else [partial]
     return pl.pallas_call(
-        functools.partial(row_kernel, bool(pieces)),
-        out_shape=outs,
-        in_specs=[scalar] * 3 + [whole] * (6 + len(pieces)),
-        out_specs=[whole] * len(outs),
-        scratch_shapes=[
-            pltpu.VMEM((2, edge + SUBLANES, edge + extent), jnp.float32),
-            pltpu.VMEM((2, edge + SUBLANES, edge + extent), jnp.float32),
-        ],
+        functools.partial(finish_kernel, block),
+        grid=(1,),
+        out_shape=jax.ShapeDtypeStruct((2, edge, edge), jnp.float32),
+        in_specs=[SCALAR] + [WHOLE] * 5 + [pl.BlockSpec(memory_space=pl.ANY)] * len(earlier),
+        out_specs=column,
+        input_output_aliases={6: 0} if earlier else {},
         cost_estimate=pl.CostEstimate(
-            flops=slots * 32 * extent**3, bytes_accessed=8 * edge * edge, transcendentals=0
+            flops=4 * edge * edge, bytes_accessed=12 * edge * edge, transcendentals=0
         ),
-        compiler_params=pltpu.CompilerParams(vmem_limit_bytes=40 << 20),
-    )(corners, counts, plane_index, tile, margin, probe, patterns, *table_set, *pieces)
-
-
-def finish_kernel(plane_index, tile, left_own, left_other, right_own, right_other, out):
-    own = plane_index[0]
-    extent = left_own.shape[1]
-    for plane, pieces in ((own, (left_own, right_own)), (1 - own, (left_other, right_other))):
-        for block, piece in enumerate(pieces):
-            cols = slice(block * extent, (block + 1) * extent)
-            step = LEARNING_RATE * piece[...].astype(jnp.float32)
-            out[plane, :, cols] = tile[plane, :, cols] - step
-
-
-def finish(plane_index, tile, pieces):
-    whole = pl.BlockSpec(memory_space=VMEM)
-    return pl.pallas_call(
-        finish_kernel,
-        out_shape=jax.ShapeDtypeStruct(tile.shape, jnp.float32),
-        in_specs=[pl.BlockSpec(memory_space=SMEM)] + [whole] * 5,
-        out_specs=whole,
-    )(plane_index, tile, *pieces)
+        compiler_params=pltpu.CompilerParams(vmem_limit_bytes=LIMIT),
+    )(plane_index, extended, *pieces, *earlier)
 
 
 def tile_pairs(count, row_shift, col_shift, grid_rows):
@@ -249,6 +294,23 @@
     return lax.ppermute(value, ("tile", "pos"), both)
 
 
+def total_wide(*values):
+    return sum(value.astype(jnp.float32) for value in values)
+
+
+def total(*values):
+    return total_wide(*values).astype(jnp.bfloat16)
+
+
+def share(keep, send, here, sharers):
+    got = [move(value, here, sharers, 1) for value in send]
+    pair = [total(*values) for values in zip(keep, got)]
+    far = [move(value, here, sharers, 3) for value in pair]
+    own = [total(*values) for values in zip(pair, far)]
+    other = [move(value, here, sharers, 1) for value in own]
+    return own, other
+
+
 def row_shards(object_tile, probe, patterns, corners, counts, table_set):
     tile_count = lax.axis_size("tile")
     sharers = lax.axis_size("pos")
@@ -256,36 +318,33 @@
     here = [(tile, tile) for tile in range(tile_count)]
     onward = tile_pairs(tile_count, 0, 1, 1)
     back = tile_pairs(tile_count, 0, -1, 1)
-    plane_index = (lax.axis_index("pos") % 2).reshape(1).astype(jnp.int32)
+    pos = lax.axis_index("pos")
+    plane_index = ((pos ^ (pos // 2)) % 2).reshape(1).astype(jnp.int32)
     margin = move(object_tile[:, :, :extent].astype(jnp.bfloat16), back, sharers, 0)
-    total = lambda *values: sum(value.astype(jnp.float32) for value in values).astype(jnp.bfloat16)
-    pieces = ()
+    edge = object_tile.shape[1]
+    extended, grad, held = load_step(corners, counts, object_tile, probe, patterns, table_set)
+    margins = [margin]
     for repeat in range(ITERS):
-        left_send, left_keep, margin_send, margin_cross, right_send, right_keep, *rest = row_step(
-            corners, counts, plane_index, object_tile, margin, probe, patterns, table_set, pieces
-        )
-        if rest:
-            object_tile = rest[0]
-        left_got = move(left_send, here, sharers, 1)
-        cross_got = move(margin_cross, onward, sharers, 1)
+        extended, grad, margin_send, halves = outer_step(
+            corners, counts, plane_index, held, extended, grad, edge, margins
+        )
+        left_keep, left_send, right_keep, right_send = (halves[i : i + 2] for i in range(0, 8, 2))
         margin_got = move(margin_send, onward, sharers, 0)
-        right_got = move(right_send, here, sharers, 1)
-        left_pair = total(left_keep, left_got, margin_got, cross_got)
-        left_far = move(left_pair, here, sharers, 2)
-        right_pair = total(right_keep, right_got)
-        right_far = move(right_pair, here, sharers, 2)
-        left_own = total(left_pair, left_far)
-        left_other = move(left_own, here, sharers, 1)
-        last = repeat == ITERS - 1
-        if not last:
-            margin_own = move(left_own, back, sharers, 0)
-            margin_other = move(left_own, back, sharers, 1)
-        right_own = total(right_pair, right_far)
-        right_other = move(right_own, here, sharers, 1)
-        pieces = (left_own, left_other, right_own, right_other)
-        if not last:
-            pieces += (margin_own, margin_other)
-    return finish(plane_index, object_tile, pieces)
+        right_own, right_other = share(right_keep, right_send, here, sharers)
+        own_got, other_got = (
+            [margin_got[plane, rows : rows + extent] for rows in (0, extent)] for plane in (0, 1)
+        )
+        left_keep = [total_wide(*pair) for pair in zip(left_keep, own_got)]
+        left_send = [total(*pair) for pair in zip(left_send, other_got)]
+        left_own, left_other = share(left_keep, left_send, here, sharers)
+        if repeat < ITERS - 1:
+            margins = [move(value, back, sharers, 0) for value in (*left_own, *left_other)]
+            pieces = (*left_own, *right_own, *left_other, *right_other)
+            extended, grad = inner_step(
+                corners, counts, plane_index, held, extended, grad, edge, pieces
+            )
+    refined = finish(plane_index, extended, edge, (*right_own, *right_other), 1, None)
+    return finish(plane_index, extended, edge, (*left_own, *left_other), 0, refined)
 
 
 def plain_kernel(corners, counts, extended, probe, patterns, first, second, out, *scratch):
@@ -293,7 +352,8 @@
     rows = extended.shape[1]
     padded[:, :rows, :] = extended[...]
     grad[...] = jnp.zeros_like(grad)
-    visit_slots(corners, counts, probe, patterns, first, second, padded, grad)
+    every = lambda col_at: col_at >= 0
+    visit_slots(every, corners, counts, probe, patterns, first, second, padded, grad)
     out[...] = grad[:, :rows, :]
 
 

time: 155 us -> 123 us (0.79)
  waiting for transfers between devices: 85.5 us -> 32.8 us
  starting transfers between devices: 32.4 us -> 55.9 us
  local copies, waits for them, and re-layouts: 8.67 us -> 2.03 us
  Pallas kernels: 26.9 us -> 29.7 us
    ppermute x19 -> x31, waiting for transfers between devices: 85.5 us -> 32.8 us  [move(): return lax.ppermute(value, ('tile', 'pos'), both)]
    ppermute x19 -> x31, starting transfers between devices: 32.4 us -> 55.9 us  [move(): return lax.ppermute(value, ('tile', 'pos'), both)]
    unnamed x21 -> x1, local copies, waits for them, and re-layouts: 7.4 us -> 0.76 us
    pallas_call x3 -> x6, Pallas kernels: 26.9 us -> 29.7 us  [the longest x2 20.3 us: outer_step(): pl.pallas_call(functools.partial(outer_kernel, edge), out_shape=outs, in_...]
  transfers between devices with their start and end apart: 19 -> 31, of which waited for: 16 -> 15; matrix products, arithmetic and copies ran while one was open for 1% -> 1% of each run, Pallas kernels for 0% -> 7%
where the time goes in v2:
time: 123 us; the launch traced here: 122 us
  starting transfers between devices  55.9 us (45%)
  waiting for transfers between devices  32.8 us (27%)
  Pallas kernels  29.7 us (24%)
  local copies, waits for them, and re-layouts  2.03 us (2%)
    ppermute x31, starting transfers between devices, move(): return lax.ppermute(value, ('tile', 'pos'), both)  55.9 us
    ppermute x31, waiting for transfers between devices, move(): return lax.ppermute(value, ('tile', 'pos'), both)  32.8 us
    pallas_call x2, Pallas kernels, outer_step(): pl.pallas_call(functools.partial(outer_kernel, edge), out_shape=outs, in_...  20.3 us
    pallas_call x1, Pallas kernels, load_step(): pl.pallas_call(functools.partial(load_kernel, edge), out_shape=[image, im...  4.53 us
    pallas_call x1, Pallas kernels, inner_step(): pl.pallas_call(functools.partial(inner_kernel, edge), out_shape=[jax.Shap...  2.71 us
  transfers between devices with their start and end apart: 31, of which 15 were waited for; matrix products, arithmetic and copies ran while one was open for 1% of the time, Pallas kernels for 7%

profile of v2, /device:TPU:0, one launch (start us, length us, event | category | flops | bytes accessed | tf_op | source)
XLA Modules:
  0.0 122.1 jit_solution(17597546741063878004)
XLA Ops:
  0.0 1.3 %slice.71 = bf16[2,512,256]{2,1,0:T(8,128)(2,1)S(1)} slice(f32[2,512,512]{2,1,0:T(8,128)} %bitcast.43), slice={[0:2], [0:512], [0:256]} | slice | bytes 1048576 | tf_op jit(solution)/shard_map/slice | solution.py:323
  1.3 5.3 %collective-permute-start = (bf16[2,512,256]{2,1,0:T(8,128)(2,1)S(1)}, bf16[2,512,256]{2,1,0:T(8,128)(2,1)S(1)}, u32[]{:S(2)}, u32[]{:S(2)}) collective-permute-start(bf16[2,512,256]{2,1,0:T(8,128)(2,1)S(1)} %slice.71), channel_id=1, source_target_pairs={{0,28},{1,29},{2,30},{3,31},{4,0},{5,1},{6,2},{7,3},{8,4},{9,5},{1... | collective-permute-start | bytes 1572872 | tf_op jit(solution)/shard_map/ppermute | solution.py:294
  7.2 0.8 copy.18.corners
  8.0 4.5 %shard_map.73 = (f32[2,520,768]{2,1,0:T(8,128)S(1)}, f32[2,520,768]{2,1,0:T(8,128)S(1)}, f32[2,256,256]{2,1,0:T(8,128)S(1)}, bf16[8,256,256]{2,1,0:T(8,128)(2,1)...) custom-call(s32[8,2]{1,0:T(8,128)S(1)} %copy.18.corners, s32[1]{0:T(128)S(6)} %copy.26.counts, ...), custom_call_target="tpu_custom_call" | custom-call | flops 2147483648 | bytes 4194304 | tf_op jit(solution)/shard_map/pallas_call | solution.py:204
  12.5 0.7 collective-permute-done.rest_6_
  13.2 10.1 %shard_map.74 = (f32[2,520,768]{2,1,0:T(8,128)S(1)}, f32[2,520,768]{2,1,0:T(8,128)S(1)}, bf16[2,512,256]{2,1,0:T(8,128)(2,1)S(1)}, f32[256,256]{1,0:T(8,128)S(1)...) custom-call(s32[8,2]{1,0:T(8,128)S(1)} %copy.18.corners, ...), custom_call_target="tpu_custom_call", output_to_operand_aliasing={{0}: (7, {}), {1}: (8, {})} | custom-call | flops 2147483648 | bytes 4194304 | tf_op jit(solution)/shard_map/pallas_call | solution.py:235
  23.3 1.9 %collective-permute-start.1 = (bf16[2,512,256]{2,1,0:T(8,128)(2,1)S(1)}, bf16[2,512,256]{2,1,0:T(8,128)(2,1)S(1)}, u32[]{:S(2)}, u32[]{:S(2)}) collective-permute-start(bf16[2,512,256]{2,1,0:T(8,128)(2,1)S(1)} %get-tuple-element.43), channel_id=1, source_target_pairs={{0,4},{1,5},{2,6},{3,7},{4,8},{5,9},{6,10},{7,11},{8,12},{9,13},{1... | collective-permute-start | bytes 1572872 | tf_op jit(solution)/shard_map/ppermute | solution.py:294
  25.3 0.1 collective-permute-start.6
  25.3 2.0 %collective-permute-start.8 = (bf16[256,256]{1,0:T(8,128)(2,1)S(1)}, bf16[256,256]{1,0:T(8,128)(2,1)S(1)}, u32[]{:S(2)}, u32[]{:S(2)}) collective-permute-start(bf16[256,256]{1,0:T(8,128)(2,1)S(1)} %get-tuple-element.50), channel_id=1, source_target_pairs={{0,1},{1,0},{2,3},{3,2},{4,5},{5,4},{6,7},{7,6},{8,9},{9,8},{10,11... | collective-permute-start | bytes 393224 | tf_op jit(solution)/shard_map/ppermute | solution.py:294
  27.4 2.9 %collective-permute-done.6 = bf16[256,256]{1,0:T(8,128)(2,1)S(1)} collective-permute-done((bf16[256,256]{1,0:T(8,128)(2,1)S(1)}, bf16[256,256]{1,0:T(8,128)(2,1)S(1)}, u32[]{:S(2)}, u32[]{:S(2)}) %collective-permute-start.6) | collective-permute-done | bytes 131104 | tf_op jit(solution)/shard_map/ppermute | solution.py:294
  30.3 2.6 %collective-permute-start.7 = (bf16[256,256]{1,0:T(8,128)(2,1)S(1)}, bf16[256,256]{1,0:T(8,128)(2,1)S(1)}, u32[]{:S(2)}, u32[]{:S(2)}) collective-permute-start(bf16[256,256]{1,0:T(8,128)(2,1)S(1)} %add_convert_fusion.9), channel_id=1, source_target_pairs={{0,3},{1,2},{2,1},{3,0},{4,7},{5,6},{6,5},{7,4},{8,11},{9,10},{10,... | collective-permute-start | bytes 393224 | tf_op jit(solution)/shard_map/ppermute | solution.py:294
  33.0 1.8 %collective-permute-done.1 = bf16[2,512,256]{2,1,0:T(8,128)(2,1)S(1)} collective-permute-done((bf16[2,512,256]{2,1,0:T(8,128)(2,1)S(1)}, bf16[2,512,256]{2,1,0:T(8,128)(2,1)S(1)}, u32[]{:S(2)}, u32[]{:S(2)}) %collective-permute-start.1) | collective-permute-done | bytes 524320 | tf_op jit(solution)/shard_map/ppermute | solution.py:294
  34.8 0.1 collective-permute-start.4
  34.8 0.0 collective-permute-done.8
  34.9 3.5 %collective-permute-start.9 = (bf16[256,256]{1,0:T(8,128)(2,1)S(1)}, bf16[256,256]{1,0:T(8,128)(2,1)S(1)}, u32[]{:S(2)}, u32[]{:S(2)}) collective-permute-start(bf16[256,256]{1,0:T(8,128)(2,1)S(1)} %add_convert_fusion.7), channel_id=1, source_target_pairs={{0,3},{1,2},{2,1},{3,0},{4,7},{5,6},{6,5},{7,4},{8,11},{9,10},{10,... | collective-permute-start | bytes 393224 | tf_op jit(solution)/shard_map/ppermute | solution.py:294
  38.4 3.2 %collective-permute-done.4 = bf16[256,256]{1,0:T(8,128)(2,1)S(1)} collective-permute-done((bf16[256,256]{1,0:T(8,128)(2,1)S(1)}, bf16[256,256]{1,0:T(8,128)(2,1)S(1)}, u32[]{:S(2)}, u32[]{:S(2)}) %collective-permute-start.4) | collective-permute-done | bytes 131104 | tf_op jit(solution)/shard_map/ppermute | solution.py:294
  41.6 0.1 fusion.8
  41.7 0.7 collective-permute-start.2
  42.4 1.5 %collective-permute-start.12 = (bf16[256,256]{1,0:T(8,128)(2,1)S(1)}, bf16[256,256]{1,0:T(8,128)(2,1)S(1)}, u32[]{:S(2)}, u32[]{:S(2)}) collective-permute-start(bf16[256,256]{1,0:T(8,128)(2,1)S(1)} %add_convert_fusion.8.rest_8_), channel_id=1, source_target_pairs={{0,1},{1,0},{2,3},{3,2},{4,5},{5,4},{6,7},{7,6},{8,9},{9,8},{10,11... | collective-permute-start | bytes 393224 | tf_op jit(solution)/shard_map/ppermute | solution.py:294
  43.9 0.7 collective-permute-start.5
  44.6 4.5 %collective-permute-done.2 = bf16[256,256]{1,0:T(8,128)(2,1)S(1)} collective-permute-done((bf16[256,256]{1,0:T(8,128)(2,1)S(1)}, bf16[256,256]{1,0:T(8,128)(2,1)S(1)}, u32[]{:S(2)}, u32[]{:S(2)}) %collective-permute-start.2) | collective-permute-done | bytes 131104 | tf_op jit(solution)/shard_map/ppermute | solution.py:294
  49.1 0.1 fusion.11
  49.1 0.3 collective-permute-start.3
  49.5 3.4 %collective-permute-done.5 = bf16[256,256]{1,0:T(8,128)(2,1)S(1)} collective-permute-done((bf16[256,256]{1,0:T(8,128)(2,1)S(1)}, bf16[256,256]{1,0:T(8,128)(2,1)S(1)}, u32[]{:S(2)}, u32[]{:S(2)}) %collective-permute-start.5) | collective-permute-done | bytes 131104 | tf_op jit(solution)/shard_map/ppermute | solution.py:294
  52.9 1.3 %collective-permute-start.11 = (bf16[256,256]{1,0:T(8,128)(2,1)S(1)}, bf16[256,256]{1,0:T(8,128)(2,1)S(1)}, u32[]{:S(2)}, u32[]{:S(2)}) collective-permute-start(bf16[256,256]{1,0:T(8,128)(2,1)S(1)} %add_convert_fusion.10.rest_7_), channel_id=1, source_target_pairs={{0,1},{1,0},{2,3},{3,2},{4,5},{5,4},{6,7},{7,6},{8,9},{9,8},{10,11... | collective-permute-start | bytes 393224 | tf_op jit(solution)/shard_map/ppermute | solution.py:294
  54.2 2.9 %collective-permute-done.3 = bf16[256,256]{1,0:T(8,128)(2,1)S(1)} collective-permute-done((bf16[256,256]{1,0:T(8,128)(2,1)S(1)}, bf16[256,256]{1,0:T(8,128)(2,1)S(1)}, u32[]{:S(2)}, u32[]{:S(2)}) %collective-permute-start.3) | collective-permute-done | bytes 131104 | tf_op jit(solution)/shard_map/ppermute | solution.py:294
  57.2 0.2 collective-permute-start.10
  57.4 2.0 %collective-permute-start.13 = (bf16[256,256]{1,0:T(8,128)(2,1)S(1)}, bf16[256,256]{1,0:T(8,128)(2,1)S(1)}, u32[]{:S(2)}, u32[]{:S(2)}) collective-permute-start(bf16[256,256]{1,0:T(8,128)(2,1)S(1)} %add_convert_fusion.6.rest_9_), channel_id=1, source_target_pairs={{0,1},{1,0},{2,3},{3,2},{4,5},{5,4},{6,7},{7,6},{8,9},{9,8},{10,11... | collective-permute-start | bytes 393224 | tf_op jit(solution)/shard_map/ppermute | solution.py:294
  59.4 1.9 %collective-permute-start.15 = (bf16[256,256]{1,0:T(8,128)(2,1)S(1)}, bf16[256,256]{1,0:T(8,128)(2,1)S(1)}, u32[]{:S(2)}, u32[]{:S(2)}) collective-permute-start(bf16[256,256]{1,0:T(8,128)(2,1)S(1)} %add_convert_fusion.10.rest_7_), channel_id=1, source_target_pairs={{0,28},{1,29},{2,30},{3,31},{4,0},{5,1},{6,2},{7,3},{8,4},{9,5},{1... | collective-permute-start | bytes 393224 | tf_op jit(solution)/shard_map/ppermute | solution.py:294
  61.3 0.0 collective-permute-done.12.rest_12_
  61.3 3.3 %collective-permute-start.14 = (bf16[256,256]{1,0:T(8,128)(2,1)S(1)}, bf16[256,256]{1,0:T(8,128)(2,1)S(1)}, u32[]{:S(2)}, u32[]{:S(2)}) collective-permute-start(bf16[256,256]{1,0:T(8,128)(2,1)S(1)} %add_convert_fusion.11.rest_6_), channel_id=1, source_target_pairs={{0,28},{1,29},{2,30},{3,31},{4,0},{5,1},{6,2},{7,3},{8,4},{9,5},{1... | collective-permute-start | bytes 393224 | tf_op jit(solution)/shard_map/ppermute | solution.py:294
  64.6 0.0 collective-permute-done.11.rest_11_
  64.6 1.9 %collective-permute-start.17 = (bf16[256,256]{1,0:T(8,128)(2,1)S(1)}, bf16[256,256]{1,0:T(8,128)(2,1)S(1)}, u32[]{:S(2)}, u32[]{:S(2)}) collective-permute-start(bf16[256,256]{1,0:T(8,128)(2,1)S(1)} %collective-permute-done.11.rest_11_), channel_id=1, source_target_pairs={{0,28},{1,29},{2,30},{3,31},{4,0},{5,1},{6,2},{7,3},{8,4},{9,5},{1... | collective-permute-start | bytes 393224 | tf_op jit(solution)/shard_map/ppermute | solution.py:294
  66.5 0.0 collective-permute-done.10.rest_10_
  66.5 1.9 %collective-permute-start.16 = (bf16[256,256]{1,0:T(8,128)(2,1)S(1)}, bf16[256,256]{1,0:T(8,128)(2,1)S(1)}, u32[]{:S(2)}, u32[]{:S(2)}) collective-permute-start(bf16[256,256]{1,0:T(8,128)(2,1)S(1)} %collective-permute-done.10.rest_10_), channel_id=1, source_target_pairs={{0,28},{1,29},{2,30},{3,31},{4,0},{5,1},{6,2},{7,3},{8,4},{9,5},{1... | collective-permute-start | bytes 393224 | tf_op jit(solution)/shard_map/ppermute | solution.py:294
  68.5 2.7 %shard_map.75 = (f32[2,520,768]{2,1,0:T(8,128)S(1)}, f32[2,520,768]{2,1,0:T(8,128)S(1)}) custom-call(s32[8,2]{1,0:T(8,128)S(1)} %copy.18.corners, s32[1]{0:T(128)S(6)} %copy.26.counts, s32[1]{0:T(128)} %bitcast.plane_index, f32[2,256,256]{2,1,0:T(8,128)S(1)} %get-tuple-element.34.rest_0_, ...), custom_call_target="tpu_custom_call", output_to_operand_aliasing={{0}: (7, {}), {1}: (8, {})} | custom-call | flops 2147483648 | bytes 4194304 | tf_op jit(solution)/shard_map/pallas_call | solution.py:217
  71.2 0.0 collective-permute-done.17.rest_9_
  71.2 10.2 %shard_map.76 = (f32[2,520,768]{2,1,0:T(8,128)S(1)}, f32[2,520,768]{2,1,0:T(8,128)S(1)}, bf16[2,512,256]{2,1,0:T(8,128)(2,1)S(1)}, f32[256,256]{1,0:T(8,128)S(1)...) custom-call(s32[8,2]{1,0:T(8,128)S(1)} %copy.18.corners, ...), custom_call_target="tpu_custom_call", output_to_operand_aliasing={{0}: (7, {}), {1}: (8, {})} | custom-call | flops 2147483648 | bytes 4194304 | tf_op jit(solution)/shard_map/pallas_call | solution.py:235
  81.4 0.1 collective-permute-start.25
  81.5 1.9 %collective-permute-start.18 = (bf16[2,512,256]{2,1,0:T(8,128)(2,1)S(1)}, bf16[2,512,256]{2,1,0:T(8,128)(2,1)S(1)}, u32[]{:S(2)}, u32[]{:S(2)}) collective-permute-start(bf16[2,512,256]{2,1,0:T(8,128)(2,1)S(1)} %get-tuple-element.55), channel_id=1, source_target_pairs={{0,4},{1,5},{2,6},{3,7},{4,8},{5,9},{6,10},{7,11},{8,12},{9,13},{1... | collective-permute-start | bytes 1572872 | tf_op jit(solution)/shard_map/ppermute | solution.py:294
  83.4 2.1 %collective-permute-start.27 = (bf16[256,256]{1,0:T(8,128)(2,1)S(1)}, bf16[256,256]{1,0:T(8,128)(2,1)S(1)}, u32[]{:S(2)}, u32[]{:S(2)}) collective-permute-start(bf16[256,256]{1,0:T(8,128)(2,1)S(1)} %get-tuple-element.62), channel_id=1, source_target_pairs={{0,1},{1,0},{2,3},{3,2},{4,5},{5,4},{6,7},{7,6},{8,9},{9,8},{10,11... | collective-permute-start | bytes 393224 | tf_op jit(solution)/shard_map/ppermute | solution.py:294
  85.5 1.0 collective-permute-done.25
  86.5 1.6 %collective-permute-start.26 = (bf16[256,256]{1,0:T(8,128)(2,1)S(1)}, bf16[256,256]{1,0:T(8,128)(2,1)S(1)}, u32[]{:S(2)}, u32[]{:S(2)}) collective-permute-start(bf16[256,256]{1,0:T(8,128)(2,1)S(1)} %add_convert_fusion.3), channel_id=1, source_target_pairs={{0,3},{1,2},{2,1},{3,0},{4,7},{5,6},{6,5},{7,4},{8,11},{9,10},{10,... | collective-permute-start | bytes 393224 | tf_op jit(solution)/shard_map/ppermute | solution.py:294
  88.1 1.3 %collective-permute-done.27 = bf16[256,256]{1,0:T(8,128)(2,1)S(1)} collective-permute-done((bf16[256,256]{1,0:T(8,128)(2,1)S(1)}, bf16[256,256]{1,0:T(8,128)(2,1)S(1)}, u32[]{:S(2)}, u32[]{:S(2)}) %collective-permute-start.27) | collective-permute-done | bytes 131104 | tf_op jit(solution)/shard_map/ppermute | solution.py:294
  89.4 4.0 %collective-permute-start.28 = (bf16[256,256]{1,0:T(8,128)(2,1)S(1)}, bf16[256,256]{1,0:T(8,128)(2,1)S(1)}, u32[]{:S(2)}, u32[]{:S(2)}) collective-permute-start(bf16[256,256]{1,0:T(8,128)(2,1)S(1)} %add_convert_fusion.1), channel_id=1, source_target_pairs={{0,3},{1,2},{2,1},{3,0},{4,7},{5,6},{6,5},{7,4},{8,11},{9,10},{10,... | collective-permute-start | bytes 393224 | tf_op jit(solution)/shard_map/ppermute | solution.py:294
  93.4 1.6 %collective-permute-start.21 = (bf16[256,256]{1,0:T(8,128)(2,1)S(1)}, bf16[256,256]{1,0:T(8,128)(2,1)S(1)}, u32[]{:S(2)}, u32[]{:S(2)}) collective-permute-start(bf16[256,256]{1,0:T(8,128)(2,1)S(1)} %fusion), channel_id=1, source_target_pairs={{0,1},{1,0},{2,3},{3,2},{4,5},{5,4},{6,7},{7,6},{8,9},{9,8},{10,11... | collective-permute-start | bytes 393224 | tf_op jit(solution)/shard_map/ppermute | solution.py:294
  95.0 4.2 %collective-permute-start.29 = (bf16[256,256]{1,0:T(8,128)(2,1)S(1)}, bf16[256,256]{1,0:T(8,128)(2,1)S(1)}, u32[]{:S(2)}, u32[]{:S(2)}) collective-permute-start(bf16[256,256]{1,0:T(8,128)(2,1)S(1)} %add_convert_fusion.2.own_top), channel_id=1, source_target_pairs={{0,1},{1,0},{2,3},{3,2},{4,5},{5,4},{6,7},{7,6},{8,9},{9,8},{10,11... | collective-permute-start | bytes 393224 | tf_op jit(solution)/shard_map/ppermute | solution.py:294
  99.3 1.2 collective-permute-done.21
  100.5 0.1 fusion.2
  100.5 1.3 %collective-permute-start.19 = (bf16[256,256]{1,0:T(8,128)(2,1)S(1)}, bf16[256,256]{1,0:T(8,128)(2,1)S(1)}, u32[]{:S(2)}, u32[]{:S(2)}) collective-permute-start(bf16[256,256]{1,0:T(8,128)(2,1)S(1)} %get-tuple-element.64), channel_id=1, source_target_pairs={{0,1},{1,0},{2,3},{3,2},{4,5},{5,4},{6,7},{7,6},{8,9},{9,8},{10,11... | collective-permute-start | bytes 393224 | tf_op jit(solution)/shard_map/ppermute | solution.py:294
  101.8 0.0 collective-permute-done.28
  101.8 0.9 collective-permute-start.30
  102.7 3.1 %collective-permute-start.22 = (bf16[256,256]{1,0:T(8,128)(2,1)S(1)}, bf16[256,256]{1,0:T(8,128)(2,1)S(1)}, u32[]{:S(2)}, u32[]{:S(2)}) collective-permute-start(bf16[256,256]{1,0:T(8,128)(2,1)S(1)} %get-tuple-element.63), channel_id=1, source_target_pairs={{0,3},{1,2},{2,1},{3,0},{4,7},{5,6},{6,5},{7,4},{8,11},{9,10},{10,... | collective-permute-start | bytes 393224 | tf_op jit(solution)/shard_map/ppermute | solution.py:294
  105.8 1.1 collective-permute-done.19
  107.0 2.4 %collective-permute-start.20 = (bf16[256,256]{1,0:T(8,128)(2,1)S(1)}, bf16[256,256]{1,0:T(8,128)(2,1)S(1)}, u32[]{:S(2)}, u32[]{:S(2)}) collective-permute-start(bf16[256,256]{1,0:T(8,128)(2,1)S(1)} %fusion.5), channel_id=1, source_target_pairs={{0,3},{1,2},{2,1},{3,0},{4,7},{5,6},{6,5},{7,4},{8,11},{9,10},{10,... | collective-permute-start | bytes 393224 | tf_op jit(solution)/shard_map/ppermute | solution.py:294
  109.4 4.6 %collective-permute-done.22 = bf16[256,256]{1,0:T(8,128)(2,1)S(1)} collective-permute-done((bf16[256,256]{1,0:T(8,128)(2,1)S(1)}, bf16[256,256]{1,0:T(8,128)(2,1)S(1)}, u32[]{:S(2)}, u32[]{:S(2)}) %collective-permute-start.22) | collective-permute-done | bytes 131104 | tf_op jit(solution)/shard_map/ppermute | solution.py:294
  114.0 0.1 collective-permute-start.24
  114.1 1.8 %collective-permute-done.20 = bf16[256,256]{1,0:T(8,128)(2,1)S(1)} collective-permute-done((bf16[256,256]{1,0:T(8,128)(2,1)S(1)}, bf16[256,256]{1,0:T(8,128)(2,1)S(1)}, u32[]{:S(2)}, u32[]{:S(2)}) %collective-permute-start.20) | collective-permute-done | bytes 131104 | tf_op jit(solution)/shard_map/ppermute | solution.py:294
  115.9 1.6 %collective-permute-start.23 = (bf16[256,256]{1,0:T(8,128)(2,1)S(1)}, bf16[256,256]{1,0:T(8,128)(2,1)S(1)}, u32[]{:S(2)}, u32[]{:S(2)}) collective-permute-start(bf16[256,256]{1,0:T(8,128)(2,1)S(1)} %add_convert_fusion.5.own_top), channel_id=1, source_target_pairs={{0,1},{1,0},{2,3},{3,2},{4,5},{5,4},{6,7},{7,6},{8,9},{9,8},{10,11... | collective-permute-start | bytes 393224 | tf_op jit(solution)/shard_map/ppermute | solution.py:294
  117.5 0.0 collective-permute-done.29.other_top
  117.5 1.1 shard_map.77.rest_0_
  118.6 1.0 collective-permute-done.24.other_low
  119.6 1.4 %collective-permute-done.23.other_top = bf16[256,256]{1,0:T(8,128)(2,1)S(1)} collective-permute-done((bf16[256,256]{1,0:T(8,128)(2,1)S(1)}, bf16[256,256]{1,0:T(8,128)(2,1)S(1)}, u32[]{:S(2)}, u32[]{:S(2)}) %collective-permute-start.23) | collective-permute-done | bytes 131104 | tf_op jit(solution)/shard_map/ppermute | solution.py:294
  121.0 1.1 shard_map.78
  (24 shorter events, 0.5 us)
Async XLA Ops:
  1.3 12.0 %collective-permute-start = (bf16[2,512,256]{2,1,0:T(8,128)(2,1)S(1)}, bf16[2,512,256]{2,1,0:T(8,128)(2,1)S(1)}, u32[]{:S(2)}, u32[]{:S(2)}) collective-permute-start(bf16[2,512,256]{2,1,0:T(8,128)(2,1)S(1)} %slice.71), channel_id=1, source_target_pairs={{0,28},{1,29},{2,30},{3,31},{4,0},{5,1},{6,2},{7,3},{8,4},{9,5},{1... | collective-permute-start | bytes 1572872 | tf_op jit(solution)/shard_map/ppermute | solution.py:294
  23.3 11.4 %collective-permute-start.1 = (bf16[2,512,256]{2,1,0:T(8,128)(2,1)S(1)}, bf16[2,512,256]{2,1,0:T(8,128)(2,1)S(1)}, u32[]{:S(2)}, u32[]{:S(2)}) collective-permute-start(bf16[2,512,256]{2,1,0:T(8,128)(2,1)S(1)} %get-tuple-element.43), channel_id=1, source_target_pairs={{0,4},{1,5},{2,6},{3,7},{4,8},{5,9},{6,10},{7,11},{8,12},{9,13},{1... | collective-permute-start | bytes 1572872 | tf_op jit(solution)/shard_map/ppermute | solution.py:294
  25.3 5.0 %collective-permute-start.6 = (bf16[256,256]{1,0:T(8,128)(2,1)S(1)}, bf16[256,256]{1,0:T(8,128)(2,1)S(1)}, u32[]{:S(2)}, u32[]{:S(2)}) collective-permute-start(bf16[256,256]{1,0:T(8,128)(2,1)S(1)} %get-tuple-element.48), channel_id=1, source_target_pairs={{0,1},{1,0},{2,3},{3,2},{4,5},{5,4},{6,7},{7,6},{8,9},{9,8},{10,11... | collective-permute-start | bytes 393224 | tf_op jit(solution)/shard_map/ppermute | solution.py:294
  25.3 9.5 %collective-permute-start.8 = (bf16[256,256]{1,0:T(8,128)(2,1)S(1)}, bf16[256,256]{1,0:T(8,128)(2,1)S(1)}, u32[]{:S(2)}, u32[]{:S(2)}) collective-permute-start(bf16[256,256]{1,0:T(8,128)(2,1)S(1)} %get-tuple-element.50), channel_id=1, source_target_pairs={{0,1},{1,0},{2,3},{3,2},{4,5},{5,4},{6,7},{7,6},{8,9},{9,8},{10,11... | collective-permute-start | bytes 393224 | tf_op jit(solution)/shard_map/ppermute | solution.py:294
  30.3 12.0 %collective-permute-start.7 = (bf16[256,256]{1,0:T(8,128)(2,1)S(1)}, bf16[256,256]{1,0:T(8,128)(2,1)S(1)}, u32[]{:S(2)}, u32[]{:S(2)}) collective-permute-start(bf16[256,256]{1,0:T(8,128)(2,1)S(1)} %add_convert_fusion.9), channel_id=1, source_target_pairs={{0,3},{1,2},{2,1},{3,0},{4,7},{5,6},{6,5},{7,4},{8,11},{9,10},{10,... | collective-permute-start | bytes 393224 | tf_op jit(solution)/shard_map/ppermute | solution.py:294
  34.8 6.8 %collective-permute-start.4 = (bf16[256,256]{1,0:T(8,128)(2,1)S(1)}, bf16[256,256]{1,0:T(8,128)(2,1)S(1)}, u32[]{:S(2)}, u32[]{:S(2)}) collective-permute-start(bf16[256,256]{1,0:T(8,128)(2,1)S(1)} %fusion.6), channel_id=1, source_target_pairs={{0,1},{1,0},{2,3},{3,2},{4,5},{5,4},{6,7},{7,6},{8,9},{9,8},{10,11... | collective-permute-start | bytes 393224 | tf_op jit(solution)/shard_map/ppermute | solution.py:294
  34.9 22.5 %collective-permute-start.9 = (bf16[256,256]{1,0:T(8,128)(2,1)S(1)}, bf16[256,256]{1,0:T(8,128)(2,1)S(1)}, u32[]{:S(2)}, u32[]{:S(2)}) collective-permute-start(bf16[256,256]{1,0:T(8,128)(2,1)S(1)} %add_convert_fusion.7), channel_id=1, source_target_pairs={{0,3},{1,2},{2,1},{3,0},{4,7},{5,6},{6,5},{7,4},{8,11},{9,10},{10,... | collective-permute-start | bytes 393224 | tf_op jit(solution)/shard_map/ppermute | solution.py:294
  41.7 7.4 %collective-permute-start.2 = (bf16[256,256]{1,0:T(8,128)(2,1)S(1)}, bf16[256,256]{1,0:T(8,128)(2,1)S(1)}, u32[]{:S(2)}, u32[]{:S(2)}) collective-permute-start(bf16[256,256]{1,0:T(8,128)(2,1)S(1)} %get-tuple-element.66), channel_id=1, source_target_pairs={{0,1},{1,0},{2,3},{3,2},{4,5},{5,4},{6,7},{7,6},{8,9},{9,8},{10,11... | collective-permute-start | bytes 393224 | tf_op jit(solution)/shard_map/ppermute | solution.py:294
  42.4 18.9 %collective-permute-start.12 = (bf16[256,256]{1,0:T(8,128)(2,1)S(1)}, bf16[256,256]{1,0:T(8,128)(2,1)S(1)}, u32[]{:S(2)}, u32[]{:S(2)}) collective-permute-start(bf16[256,256]{1,0:T(8,128)(2,1)S(1)} %add_convert_fusion.8.rest_8_), channel_id=1, source_target_pairs={{0,1},{1,0},{2,3},{3,2},{4,5},{5,4},{6,7},{7,6},{8,9},{9,8},{10,11... | collective-permute-start | bytes 393224 | tf_op jit(solution)/shard_map/ppermute | solution.py:294
  43.9 9.0 %collective-permute-start.5 = (bf16[256,256]{1,0:T(8,128)(2,1)S(1)}, bf16[256,256]{1,0:T(8,128)(2,1)S(1)}, u32[]{:S(2)}, u32[]{:S(2)}) collective-permute-start(bf16[256,256]{1,0:T(8,128)(2,1)S(1)} %get-tuple-element.65), channel_id=1, source_target_pairs={{0,3},{1,2},{2,1},{3,0},{4,7},{5,6},{6,5},{7,4},{8,11},{9,10},{10,... | collective-permute-start | bytes 393224 | tf_op jit(solution)/shard_map/ppermute | solution.py:294
  49.1 8.0 %collective-permute-start.3 = (bf16[256,256]{1,0:T(8,128)(2,1)S(1)}, bf16[256,256]{1,0:T(8,128)(2,1)S(1)}, u32[]{:S(2)}, u32[]{:S(2)}) collective-permute-start(bf16[256,256]{1,0:T(8,128)(2,1)S(1)} %fusion.11), channel_id=1, source_target_pairs={{0,3},{1,2},{2,1},{3,0},{4,7},{5,6},{6,5},{7,4},{8,11},{9,10},{10,... | collective-permute-start | bytes 393224 | tf_op jit(solution)/shard_map/ppermute | solution.py:294
  52.9 11.7 %collective-permute-start.11 = (bf16[256,256]{1,0:T(8,128)(2,1)S(1)}, bf16[256,256]{1,0:T(8,128)(2,1)S(1)}, u32[]{:S(2)}, u32[]{:S(2)}) collective-permute-start(bf16[256,256]{1,0:T(8,128)(2,1)S(1)} %add_convert_fusion.10.rest_7_), channel_id=1, source_target_pairs={{0,1},{1,0},{2,3},{3,2},{4,5},{5,4},{6,7},{7,6},{8,9},{9,8},{10,11... | collective-permute-start | bytes 393224 | tf_op jit(solution)/shard_map/ppermute | solution.py:294
  57.2 9.4 %collective-permute-start.10 = (bf16[256,256]{1,0:T(8,128)(2,1)S(1)}, bf16[256,256]{1,0:T(8,128)(2,1)S(1)}, u32[]{:S(2)}, u32[]{:S(2)}) collective-permute-start(bf16[256,256]{1,0:T(8,128)(2,1)S(1)} %add_convert_fusion.11.rest_6_), channel_id=1, source_target_pairs={{0,1},{1,0},{2,3},{3,2},{4,5},{5,4},{6,7},{7,6},{8,9},{9,8},{10,11... | collective-permute-start | bytes 393224 | tf_op jit(solution)/shard_map/ppermute | solution.py:294
  57.4 11.1 %collective-permute-start.13 = (bf16[256,256]{1,0:T(8,128)(2,1)S(1)}, bf16[256,256]{1,0:T(8,128)(2,1)S(1)}, u32[]{:S(2)}, u32[]{:S(2)}) collective-permute-start(bf16[256,256]{1,0:T(8,128)(2,1)S(1)} %add_convert_fusion.6.rest_9_), channel_id=1, source_target_pairs={{0,1},{1,0},{2,3},{3,2},{4,5},{5,4},{6,7},{7,6},{8,9},{9,8},{10,11... | collective-permute-start | bytes 393224 | tf_op jit(solution)/shard_map/ppermute | solution.py:294
  59.4 11.9 %collective-permute-start.15 = (bf16[256,256]{1,0:T(8,128)(2,1)S(1)}, bf16[256,256]{1,0:T(8,128)(2,1)S(1)}, u32[]{:S(2)}, u32[]{:S(2)}) collective-permute-start(bf16[256,256]{1,0:T(8,128)(2,1)S(1)} %add_convert_fusion.10.rest_7_), channel_id=1, source_target_pairs={{0,28},{1,29},{2,30},{3,31},{4,0},{5,1},{6,2},{7,3},{8,4},{9,5},{1... | collective-permute-start | bytes 393224 | tf_op jit(solution)/shard_map/ppermute | solution.py:294
  61.3 9.9 %collective-permute-start.14 = (bf16[256,256]{1,0:T(8,128)(2,1)S(1)}, bf16[256,256]{1,0:T(8,128)(2,1)S(1)}, u32[]{:S(2)}, u32[]{:S(2)}) collective-permute-start(bf16[256,256]{1,0:T(8,128)(2,1)S(1)} %add_convert_fusion.11.rest_6_), channel_id=1, source_target_pairs={{0,28},{1,29},{2,30},{3,31},{4,0},{5,1},{6,2},{7,3},{8,4},{9,5},{1... | collective-permute-start | bytes 393224 | tf_op jit(solution)/shard_map/ppermute | solution.py:294
  64.6 6.6 %collective-permute-start.17 = (bf16[256,256]{1,0:T(8,128)(2,1)S(1)}, bf16[256,256]{1,0:T(8,128)(2,1)S(1)}, u32[]{:S(2)}, u32[]{:S(2)}) collective-permute-start(bf16[256,256]{1,0:T(8,128)(2,1)S(1)} %collective-permute-done.11.rest_11_), channel_id=1, source_target_pairs={{0,28},{1,29},{2,30},{3,31},{4,0},{5,1},{6,2},{7,3},{8,4},{9,5},{1... | collective-permute-start | bytes 393224 | tf_op jit(solution)/shard_map/ppermute | solution.py:294
  66.5 4.7 %collective-permute-start.16 = (bf16[256,256]{1,0:T(8,128)(2,1)S(1)}, bf16[256,256]{1,0:T(8,128)(2,1)S(1)}, u32[]{:S(2)}, u32[]{:S(2)}) collective-permute-start(bf16[256,256]{1,0:T(8,128)(2,1)S(1)} %collective-permute-done.10.rest_10_), channel_id=1, source_target_pairs={{0,28},{1,29},{2,30},{3,31},{4,0},{5,1},{6,2},{7,3},{8,4},{9,5},{1... | collective-permute-start | bytes 393224 | tf_op jit(solution)/shard_map/ppermute | solution.py:294
  81.4 5.0 %collective-permute-start.25 = (bf16[256,256]{1,0:T(8,128)(2,1)S(1)}, bf16[256,256]{1,0:T(8,128)(2,1)S(1)}, u32[]{:S(2)}, u32[]{:S(2)}) collective-permute-start(bf16[256,256]{1,0:T(8,128)(2,1)S(1)} %get-tuple-element.60), channel_id=1, source_target_pairs={{0,1},{1,0},{2,3},{3,2},{4,5},{5,4},{6,7},{7,6},{8,9},{9,8},{10,11... | collective-permute-start | bytes 393224 | tf_op jit(solution)/shard_map/ppermute | solution.py:294
  81.5 11.9 %collective-permute-start.18 = (bf16[2,512,256]{2,1,0:T(8,128)(2,1)S(1)}, bf16[2,512,256]{2,1,0:T(8,128)(2,1)S(1)}, u32[]{:S(2)}, u32[]{:S(2)}) collective-permute-start(bf16[2,512,256]{2,1,0:T(8,128)(2,1)S(1)} %get-tuple-element.55), channel_id=1, source_target_pairs={{0,4},{1,5},{2,6},{3,7},{4,8},{5,9},{6,10},{7,11},{8,12},{9,13},{1... | collective-permute-start | bytes 1572872 | tf_op jit(solution)/shard_map/ppermute | solution.py:294
  83.4 5.9 %collective-permute-start.27 = (bf16[256,256]{1,0:T(8,128)(2,1)S(1)}, bf16[256,256]{1,0:T(8,128)(2,1)S(1)}, u32[]{:S(2)}, u32[]{:S(2)}) collective-permute-start(bf16[256,256]{1,0:T(8,128)(2,1)S(1)} %get-tuple-element.62), channel_id=1, source_target_pairs={{0,1},{1,0},{2,3},{3,2},{4,5},{5,4},{6,7},{7,6},{8,9},{9,8},{10,11... | collective-permute-start | bytes 393224 | tf_op jit(solution)/shard_map/ppermute | solution.py:294
  86.5 8.5 %collective-permute-start.26 = (bf16[256,256]{1,0:T(8,128)(2,1)S(1)}, bf16[256,256]{1,0:T(8,128)(2,1)S(1)}, u32[]{:S(2)}, u32[]{:S(2)}) collective-permute-start(bf16[256,256]{1,0:T(8,128)(2,1)S(1)} %add_convert_fusion.3), channel_id=1, source_target_pairs={{0,3},{1,2},{2,1},{3,0},{4,7},{5,6},{6,5},{7,4},{8,11},{9,10},{10,... | collective-permute-start | bytes 393224 | tf_op jit(solution)/shard_map/ppermute | solution.py:294
  89.4 12.4 %collective-permute-start.28 = (bf16[256,256]{1,0:T(8,128)(2,1)S(1)}, bf16[256,256]{1,0:T(8,128)(2,1)S(1)}, u32[]{:S(2)}, u32[]{:S(2)}) collective-permute-start(bf16[256,256]{1,0:T(8,128)(2,1)S(1)} %add_convert_fusion.1), channel_id=1, source_target_pairs={{0,3},{1,2},{2,1},{3,0},{4,7},{5,6},{6,5},{7,4},{8,11},{9,10},{10,... | collective-permute-start | bytes 393224 | tf_op jit(solution)/shard_map/ppermute | solution.py:294
  93.4 7.0 %collective-permute-start.21 = (bf16[256,256]{1,0:T(8,128)(2,1)S(1)}, bf16[256,256]{1,0:T(8,128)(2,1)S(1)}, u32[]{:S(2)}, u32[]{:S(2)}) collective-permute-start(bf16[256,256]{1,0:T(8,128)(2,1)S(1)} %fusion), channel_id=1, source_target_pairs={{0,1},{1,0},{2,3},{3,2},{4,5},{5,4},{6,7},{7,6},{8,9},{9,8},{10,11... | collective-permute-start | bytes 393224 | tf_op jit(solution)/shard_map/ppermute | solution.py:294
  95.0 22.5 %collective-permute-start.29 = (bf16[256,256]{1,0:T(8,128)(2,1)S(1)}, bf16[256,256]{1,0:T(8,128)(2,1)S(1)}, u32[]{:S(2)}, u32[]{:S(2)}) collective-permute-start(bf16[256,256]{1,0:T(8,128)(2,1)S(1)} %add_convert_fusion.2.own_top), channel_id=1, source_target_pairs={{0,1},{1,0},{2,3},{3,2},{4,5},{5,4},{6,7},{7,6},{8,9},{9,8},{10,11... | collective-permute-start | bytes 393224 | tf_op jit(solution)/shard_map/ppermute | solution.py:294
  100.5 6.4 %collective-permute-start.19 = (bf16[256,256]{1,0:T(8,128)(2,1)S(1)}, bf16[256,256]{1,0:T(8,128)(2,1)S(1)}, u32[]{:S(2)}, u32[]{:S(2)}) collective-permute-start(bf16[256,256]{1,0:T(8,128)(2,1)S(1)} %get-tuple-element.64), channel_id=1, source_target_pairs={{0,1},{1,0},{2,3},{3,2},{4,5},{5,4},{6,7},{7,6},{8,9},{9,8},{10,11... | collective-permute-start | bytes 393224 | tf_op jit(solution)/shard_map/ppermute | solution.py:294
  101.8 15.7 %collective-permute-start.30 = (bf16[256,256]{1,0:T(8,128)(2,1)S(1)}, bf16[256,256]{1,0:T(8,128)(2,1)S(1)}, u32[]{:S(2)}, u32[]{:S(2)}) collective-permute-start(bf16[256,256]{1,0:T(8,128)(2,1)S(1)} %add_convert_fusion.own_low), channel_id=1, source_target_pairs={{0,1},{1,0},{2,3},{3,2},{4,5},{5,4},{6,7},{7,6},{8,9},{9,8},{10,11... | collective-permute-start | bytes 393224 | tf_op jit(solution)/shard_map/ppermute | solution.py:294
  102.7 11.3 %collective-permute-start.22 = (bf16[256,256]{1,0:T(8,128)(2,1)S(1)}, bf16[256,256]{1,0:T(8,128)(2,1)S(1)}, u32[]{:S(2)}, u32[]{:S(2)}) collective-permute-start(bf16[256,256]{1,0:T(8,128)(2,1)S(1)} %get-tuple-element.63), channel_id=1, source_target_pairs={{0,3},{1,2},{2,1},{3,0},{4,7},{5,6},{6,5},{7,4},{8,11},{9,10},{10,... | collective-permute-start | bytes 393224 | tf_op jit(solution)/shard_map/ppermute | solution.py:294
  107.0 8.9 %collective-permute-start.20 = (bf16[256,256]{1,0:T(8,128)(2,1)S(1)}, bf16[256,256]{1,0:T(8,128)(2,1)S(1)}, u32[]{:S(2)}, u32[]{:S(2)}) collective-permute-start(bf16[256,256]{1,0:T(8,128)(2,1)S(1)} %fusion.5), channel_id=1, source_target_pairs={{0,3},{1,2},{2,1},{3,0},{4,7},{5,6},{6,5},{7,4},{8,11},{9,10},{10,... | collective-permute-start | bytes 393224 | tf_op jit(solution)/shard_map/ppermute | solution.py:294
  114.0 5.6 %collective-permute-start.24 = (bf16[256,256]{1,0:T(8,128)(2,1)S(1)}, bf16[256,256]{1,0:T(8,128)(2,1)S(1)}, u32[]{:S(2)}, u32[]{:S(2)}) collective-permute-start(bf16[256,256]{1,0:T(8,128)(2,1)S(1)} %add_convert_fusion.4.own_low), channel_id=1, source_target_pairs={{0,1},{1,0},{2,3},{3,2},{4,5},{5,4},{6,7},{7,6},{8,9},{9,8},{10,11... | collective-permute-start | bytes 393224 | tf_op jit(solution)/shard_map/ppermute | solution.py:294
  115.9 5.1 %collective-permute-start.23 = (bf16[256,256]{1,0:T(8,128)(2,1)S(1)}, bf16[256,256]{1,0:T(8,128)(2,1)S(1)}, u32[]{:S(2)}, u32[]{:S(2)}) collective-permute-start(bf16[256,256]{1,0:T(8,128)(2,1)S(1)} %add_convert_fusion.5.own_top), channel_id=1, source_target_pairs={{0,1},{1,0},{2,3},{3,2},{4,5},{5,4},{6,7},{7,6},{8,9},{9,8},{10,11... | collective-permute-start | bytes 393224 | tf_op jit(solution)/shard_map/ppermute | solution.py:294
